TPU v7x, 32 devices: a whole 2x2x4 slice. The times are simulated.
32 devices in a mesh: clip: 2 (over y), seq: 4 (over z), head: 4 (over x, core).
Axes of the slice: x: 2, y: 2, z: 4, core: 2. Of those that a mesh axis runs over, the one named last changes fastest.
Arguments:
- queries: bfloat16 [16, 4, 16, 3072], P(('clip', 'head'), 'seq'), parts along dimension 0, may hold values from -15 to 15
- attn_keys: bfloat16 [16, 4, 16, 3072], P(('clip', 'head'), 'seq'), parts along dimension 0, may hold values from -5 to 5
- attn_values: bfloat16 [16, 4, 16, 3072], P(('clip', 'head'), 'seq'), parts along dimension 0, may hold values from -5 to 5
- residual: bfloat16 [16, 4, 16, 5120], P(('clip', 'head'), 'seq'), parts along dimension 0, may hold values from -6 to 6
- out_weight: bfloat16 [3072, 5120], P('head', 'seq'), may hold values from -0.109375 to 0.109375
- out_gate: float32 [5120], replicated, may hold values from 0.3 to 3
- head_shift: float32 [5120], replicated, may hold values from -3 to 3
- head_scale: float32 [5120], replicated, may hold values from -1.5 to 1.5
- head_weight: bfloat16 [5120, 64], replicated, may hold values from -0.078125 to 0.078125
- head_bias: float32 [64], replicated, may hold values from -3 to 3
- conv_weight: bfloat16 [3, 3, 3, 16, 384], replicated, may hold values from -0.3125 to 0.3125
- conv_bias: float32 [384], replicated, may hold values from -3 to 3
- norm_gain: float32 [384], replicated, may hold values from 0.5 to 2
Outputs:
- hidden: bfloat16 [16, 4, 16, 5120], P(('clip', 'head'), 'seq'), parts along dimension 0
- features: bfloat16 [16, 8, 32, 384], P(('clip', 'head'), 'seq'), parts along dimension 0
There are 2 independent parts, one for each index of `clip`. A program takes and returns all parts, laid end to end along the dimension named above; an argument that names none is the same for every part. Nothing has to cross between parts.
All inputs are finite; a program needn't handle non-finite values.
Results may differ from a plain program's by a relative error of at most 0.013.
Values may be sent and summed in bfloat16 or wider, within the bound.
No kernel may reach another device: no remote copies, remote signals or barrier semaphores. Data moves between devices by JAX's collectives and lax.ppermute only.
A program may use at most 128 MiB of HBM per device.

v0:
```python
import jax
import jax.numpy as jnp
from jax import lax
from jax.sharding import PartitionSpec as P

HEAD_DIM = 128


def from_behind(value, axis, steps):
    count = lax.axis_size(axis)
    first, last = (max(0, -steps), min(count, count - steps))
    return lax.ppermute(value, axis, [(source, source + steps) for source in range(first, last)])


def padded_2(x, sides, width):
    for axis, dim in sides:
        peers, length = (lax.axis_size(axis), x.shape[dim])
        up = [(i, (i + 1) % peers) for i in range(peers - 1)]
        down = [(j, i) for i, j in up]
        last = lax.slice_in_dim(x, length - width, length, axis=dim)
        first = lax.slice_in_dim(x, 0, width, axis=dim)
        before = lax.ppermute(last, axis, up)
        after = lax.ppermute(first, axis, down)
        x = jnp.concatenate([before, x, after], axis=dim)
    return x


def head_latent(hidden, head_shift, head_scale, head_weight, head_bias):
    values = hidden.astype(jnp.float32)
    center = values - jnp.mean(values, -1, keepdims=True)
    spread = jnp.mean(center * center, -1, keepdims=True)
    normed = (center * lax.rsqrt(spread + 1e-06) * (1.0 + head_scale) + head_shift).astype(
        jnp.bfloat16
    )
    flat = normed.reshape(-1, normed.shape[-1])
    latent = (jnp.dot(flat, head_weight, preferred_element_type=jnp.float32) + head_bias).astype(
        jnp.bfloat16
    )
    frames, height, breadth = (hidden.shape[0], hidden.shape[1], hidden.shape[2])
    channels = head_weight.shape[1] // 4
    patches = latent.reshape(frames, height, breadth, 2, 2, channels).transpose(0, 1, 3, 2, 4, 5)
    return patches.reshape(frames, height * 2, breadth * 2, channels)


def convolve(padded, frames, conv_weight, conv_bias, norm_gain):
    height = padded.shape[1] - 2
    breadth = padded.shape[2] - 2
    stacked = jnp.concatenate(
        [
            padded[
                time_off : time_off + frames,
                row_off : row_off + height,
                col_off : col_off + breadth,
            ]
            for time_off in range(3)
            for row_off in range(3)
            for col_off in range(3)
        ],
        -1,
    )
    kernel = conv_weight.reshape(-1, conv_weight.shape[-1])
    linear = (
        jnp.dot(stacked.reshape(-1, stacked.shape[-1]), kernel, preferred_element_type=jnp.float32)
        + conv_bias
    )
    normed = linear * lax.rsqrt(jnp.mean(linear * linear, -1, keepdims=True) + 1e-06) * norm_gain
    return jax.nn.silu(normed).astype(jnp.bfloat16).reshape(frames, height, breadth, -1)


def attend_block(carried, block_keys, block_values, query_heads):
    running, denominator, weighted = carried
    scores = jnp.einsum("hqd,khd->hqk", query_heads, block_keys, preferred_element_type=jnp.float32)
    scores = scores * query_heads.shape[-1] ** (-0.5)
    newmax = jnp.maximum(running, jnp.max(scores, -1))
    factor = jnp.exp(running - newmax)
    weights = jnp.exp(scores - newmax[..., None])
    denominator = denominator * factor + jnp.sum(weights, -1)
    product = jnp.einsum(
        "hqk,khd->hqd",
        weights.astype(jnp.bfloat16),
        block_values,
        preferred_element_type=jnp.float32,
    )
    weighted = weighted * factor[..., None] + product
    return (newmax, denominator, weighted)


def fold_pieces(query_heads, carried, pieces):
    key_piece, value_piece = pieces
    frames, height, breadth = (key_piece.shape[0], key_piece.shape[1], key_piece.shape[2])
    heads_here, head_width = (query_heads.shape[0], query_heads.shape[2])
    group_rows = 4

    def regroup(one_piece):
        shaped = one_piece.reshape(
            frames, height // group_rows, group_rows, breadth, heads_here, head_width
        )
        shaped = shaped.transpose(1, 0, 2, 3, 4, 5)
        return shaped.reshape(
            height // group_rows, frames * group_rows * breadth, heads_here, head_width
        )

    def advance(inner, blocks):
        return (attend_block(inner, blocks[0], blocks[1], query_heads), None)

    carried, _ = lax.scan(advance, carried, (regroup(key_piece), regroup(value_piece)))
    return carried


def on_device(
    queries,
    attn_keys,
    attn_values,
    residual,
    out_weight,
    out_gate,
    head_shift,
    head_scale,
    head_weight,
    head_bias,
    conv_weight,
    conv_bias,
    norm_gain,
):
    head_count = lax.axis_size("head")
    frames_dev = queries.shape[0]
    group_width = queries.shape[3] // head_count
    head_width = HEAD_DIM
    heads_here = group_width // head_width
    local_queries, local_keys, local_values = (
        lax.all_to_all(queries, "head", split_axis=3, concat_axis=0, tiled=True),
        lax.all_to_all(attn_keys, "head", split_axis=3, concat_axis=0, tiled=True),
        lax.all_to_all(attn_values, "head", split_axis=3, concat_axis=0, tiled=True),
    )
    frames_all, height, breadth = (
        local_queries.shape[0],
        local_queries.shape[1],
        local_queries.shape[2],
    )
    count = frames_all * height * breadth
    query_heads = local_queries.reshape(count, heads_here, head_width).transpose(1, 0, 2)
    initial = (
        jnp.full((heads_here, count), -1e30, jnp.float32),
        jnp.zeros((heads_here, count), jnp.float32),
        jnp.zeros((heads_here, count, head_width), jnp.float32),
    )
    carried = fold_pieces(
        query_heads,
        initial,
        (
            lax.all_gather(local_keys, "seq", axis=1, tiled=True),
            lax.all_gather(local_values, "seq", axis=1, tiled=True),
        ),
    )
    running, denominator, weighted = carried
    attended = (weighted / denominator[..., None]).astype(jnp.bfloat16)
    attended = attended.transpose(1, 0, 2).reshape(count, group_width)
    partial_value = jnp.dot(
        attended,
        lax.all_gather(out_weight, "seq", axis=1, tiled=True),
        preferred_element_type=jnp.float32,
    )
    partial_value = partial_value.reshape(frames_all, height, breadth, partial_value.shape[-1])
    owned = lax.psum_scatter(
        partial_value.astype(jnp.bfloat16), "head", scatter_dimension=0, tiled=True
    ).astype(jnp.float32)
    hidden = (residual.astype(jnp.float32) + out_gate * owned).astype(jnp.bfloat16)
    own_video = head_latent(hidden, head_shift, head_scale, head_weight, head_bias)
    earlier = from_behind(own_video, "head", 1)
    video = jnp.concatenate([earlier, own_video], 0)
    extended = padded_2(video, (("seq", 1),), 1)
    padded = jnp.pad(extended, ((0, 0), (0, 0), (1, 1), (0, 0)))
    features = convolve(padded, frames_dev, conv_weight, conv_bias, norm_gain)
    return (hidden, features)


def solution(mesh):
    return jax.shard_map(
        on_device,
        mesh=mesh,
        in_specs=(
            P(("clip", "head"), "seq", None, None),
            P(("clip", "head"), "seq", None, None),
            P(("clip", "head"), "seq", None, None),
            P(("clip", "head"), "seq", None, None),
            P("head", "seq"),
            P(),
            P(),
            P(),
            P(),
            P(),
            P(),
            P(),
            P(),
        ),
        out_specs=(P(("clip", "head"), "seq", None, None), P(("clip", "head"), "seq", None, None)),
        check_vma=False,
    )
```

profile of v0, /device:TPU:0, one launch (start us, length us, event | category | flops | bytes accessed | tf_op | source)
XLA Modules:
  0.0 232.0 jit_solution(3632974338613475676)
XLA Ops:
  7.2 0.0 copy-start
  7.2 0.0 all-gather.2.cloned.1.call-start
  7.2 0.7 all-gather.2.cloned.1.call-update
  7.9 0.2 copy-done.5
  8.2 1.8 copy.79
  10.0 2.3 reshape.122
  12.3 4.2 %all-to-all-start.1 = ((bf16[4,2,12288]{2,1,0:T(2,128)(2,1)}), bf16[4,2,12288]{2,1,0:T(2,128)(2,1)S(1)}, u32[]{:S(2)}, u32[]{:S(2)}) async-start(bf16[4,2,12288]{2,1,0:T(2,128)(2,1)} %reshape.122), calls=%async_computation.1 | async-start | bytes 393216 | tf_op jit(solution)/shard_map/all_to_all | solution.py:132
  16.5 1.8 copy.75
  18.3 0.0 copy-start.7
  18.3 2.3 reshape.124
  20.6 1.2 all-to-all-done.1
  21.8 3.4 %all-to-all-start = ((bf16[4,2,12288]{2,1,0:T(2,128)(2,1)}), bf16[4,2,12288]{2,1,0:T(2,128)(2,1)S(1)}, u32[]{:S(2)}, u32[]{:S(2)}) async-start(bf16[4,2,12288]{2,1,0:T(2,128)(2,1)} %reshape.124), calls=%async_computation | async-start | bytes 393216 | tf_op jit(solution)/shard_map/all_to_all | solution.py:131
  25.2 1.8 copy.84
  27.0 2.3 reshape.126
  29.3 1.2 reshape.123
  30.5 1.1 copy.93
  31.6 0.0 all-to-all-done
  31.6 4.0 %all-to-all-start.2 = ((bf16[4,2,12288]{2,1,0:T(2,128)(2,1)}), bf16[4,2,12288]{2,1,0:T(2,128)(2,1)}, u32[]{:S(2)}, u32[]{:S(2)}) async-start(bf16[4,2,12288]{2,1,0:T(2,128)(2,1)} %reshape.126), calls=%async_computation.2 | async-start | bytes 393216 | tf_op jit(solution)/shard_map/all_to_all | solution.py:133
  35.6 0.0 reduce-scatter.2.cloned.1.call-start
  35.7 35.5 %all_gather.9 = bf16[8,4,16,768]{3,2,0,1:T(8,128)(2,1)S(1)} all-gather(bf16[8,1,16,768]{3,2,0,1:T(8,128)(2,1)S(1)} %bitcast.111), channel_id=1, replica_groups=mesh['clip'=2,'seq'=4,'head'=4] {'seq'}, dimensions={1}, use_global_device_ids=true | all-gather | bytes 983040 | tf_op jit(solution)/shard_map/all_gather | solution.py:151
  71.2 0.1 copy.82
  71.2 0.9 squeeze.9
  72.1 1.2 reshape.125
  73.3 1.1 copy.92
  74.4 0.2 reshape.115
  74.7 5.6 %reshape.127 = bf16[3072,1,2,16]{3,2,1,0:T(2,128)(2,1)S(1)} reshape(bf16[4,2,12288]{2,1,0:T(2,128)(2,1)} %all-to-all-done.2) | data formatting | bytes 393216
  80.2 2.5 %copy.94 = bf16[2,1,16,4,768]{4,3,2,0,1:T(4,128)(2,1)} copy(bf16[2,1,16,4,768]{2,0,4,3,1:T(2,128)(2,1)S(1)} %bitcast.95) | data formatting | bytes 393216 | tf_op jit(solution)/shard_map/all_to_all | solution.py:133
  82.7 1.0 copy.86
  83.7 32.6 %all_gather.10 = bf16[8,4,16,768]{3,2,0,1:T(8,128)(2,1)S(1)} all-gather(bf16[8,1,16,768]{3,2,0,1:T(8,128)(2,1)S(1)} %bitcast.112), channel_id=1, replica_groups=mesh['clip'=2,'seq'=4,'head'=4] {'seq'}, dimensions={1}, use_global_device_ids=true | all-gather | bytes 983040 | tf_op jit(solution)/shard_map/all_gather | solution.py:152
  116.3 0.1 copy.87
  116.3 1.9 squeeze.10
  118.2 0.5 fusion.35
  118.7 0.5 fusion.8
  119.3 0.2 copy-done.2
  119.5 0.6 fusion.12
  120.1 0.1 copy.89
  120.2 0.2 dot_general.24
  120.5 0.0 copy-start.9
  120.5 0.0 copy-start.10
  120.5 57.9 %all-gather.2.cloned.1.call-done = bf16[768,5120]{1,0:T(8,128)(2,1)} async-done(((bf16[768,1280]{1,0:T(8,128)(2,1)}), bf16[768,5120]{1,0:T(8,128)(2,1)}) %all-gather.2.cloned.1.call-update) | async-done | bytes 7864336 | tf_op jit(solution)/shard_map/all_gather | solution.py:160
  178.5 5.6 %fusion.5 = bf16[8,1,16,5120]{3,2,0,1:T(8,128)(2,1)} fusion(bf16[8,16,768]{2,1,0:T(8,128)(2,1)S(1)} %dot_general.24, bf16[768,5120]{1,0:T(8,128)(2,1)} %all-gather.2.cloned.1.call-done), kind=kOutput, calls=%fused_computation.3 | convolution fusion | flops 1007288320 | bytes 9371648 | tf_op jit(solution)/shard_map/dot_general | solution.py:158
  184.1 0.0 reduce-scatter.2.cloned.1.call-update
  184.1 24.8 %reduce-scatter.2.cloned.1.call-done = bf16[2,1,16,5120]{3,2,0,1:T(8,128)(2,1)} async-done(((bf16[8,1,16,5120]{3,2,0,1:T(8,128)(2,1)}), bf16[2,1,16,5120]{3,2,0,1:T(8,128)(2,1)}) %reduce-scatter.2.cloned.1.call-update) | async-done | bytes 327696 | tf_op jit(solution)/shard_map/reduce_scatter | solution.py:164
  208.9 1.2 convert_reduce_fusion
  210.1 0.2 fusion.20
  210.4 0.0 copy-done.8
  210.4 0.2 fusion.23
  210.6 0.3 fusion.13
  210.9 0.1 reshape.117
  211.0 1.6 collective-permute-start
  212.6 0.8 collective-permute-done
  213.5 3.4 %collective-permute-start.1 = (bf16[4,1,32,16]{3,2,1,0:T(8,128)(2,1)S(1)}, bf16[4,1,32,16]{3,2,1,0:T(8,128)(2,1)S(1)}, u32[]{:S(2)}, u32[]{:S(2)}) collective-permute-start(bf16[4,1,32,16]{3,2,1,0:T(8,128)(2,1)S(1)} %get-tuple-element.63), channel_id=1, source_target_pairs={{0,4},{4,8},{8,12},{1,5},{5,9},{9,13},{2,6},{6,10},{10,14},{3,7},{... | collective-permute-start | bytes 12296 | tf_op jit(solution)/shard_map/ppermute | solution.py:22
  216.9 1.3 collective-permute-start.2
  218.2 0.3 collective-permute-done.1
  218.5 4.5 %collective-permute-done.2 = bf16[4,1,32,16]{3,2,1,0:T(8,128)(2,1)S(1)} collective-permute-done((bf16[4,1,32,16]{3,2,1,0:T(8,128)(2,1)S(1)}, bf16[4,1,32,16]{3,2,1,0:T(8,128)(2,1)S(1)}, u32[]{:S(2)}, u32[]{:S(2)}) %collective-permute-start.2) | collective-permute-done | bytes 4128 | tf_op jit(solution)/shard_map/ppermute | solution.py:23
  223.0 0.1 select_maximum_fusion
  223.0 0.0 copy-start.3
  223.1 0.0 copy-start.11
  223.1 0.0 copy-start.12
  223.1 0.1 fusion.32
  223.3 0.3 concatenate.105
  223.6 0.4 copy-done.3
  224.0 0.3 multiply_reduce_fusion
  224.4 0.8 multiply_convert_fusion
  (31 shorter events, 0.2 us)
Async XLA Ops:
  7.2 203.4 %copy-start = (bf16[5120,64]{0,1:T(8,128)(2,1)S(1)}, bf16[5120,64]{0,1:T(8,128)(2,1)}, u32[]{:S(2)}) copy-start(bf16[5120,64]{0,1:T(8,128)(2,1)} %param.21) | copy-start | bytes 1966084
  7.2 1.0 copy-start.5
  7.2 171.3 %all-gather.2.cloned.1.call-start = ((), (), s32[]{:S(2)}) async-start(), calls=%async_computation.4 | async-start | bytes 9830400 | tf_op jit(solution)/shard_map/all_gather | solution.py:160
  8.2 8.3 %copy-start.6 = (bf16[2,1,16,3072]{3,2,1,0:T(8,128)(2,1)S(1)}, bf16[2,1,16,3072]{3,2,1,0:T(8,128)(2,1)}, u32[]{:S(2)}) copy-start(bf16[2,1,16,3072]{3,2,1,0:T(8,128)(2,1)} %param.13) | copy-start | bytes 589828
  12.3 9.5 %all-to-all-start.1 = ((bf16[4,2,12288]{2,1,0:T(2,128)(2,1)}), bf16[4,2,12288]{2,1,0:T(2,128)(2,1)S(1)}, u32[]{:S(2)}, u32[]{:S(2)}) async-start(bf16[4,2,12288]{2,1,0:T(2,128)(2,1)} %reshape.122), calls=%async_computation.1 | async-start | bytes 393216 | tf_op jit(solution)/shard_map/all_to_all | solution.py:132
  18.3 6.9 %copy-start.7 = (bf16[2,1,16,3072]{3,2,1,0:T(8,128)(2,1)S(1)}, bf16[2,1,16,3072]{3,2,1,0:T(8,128)(2,1)}, u32[]{:S(2)}) copy-start(bf16[2,1,16,3072]{3,2,1,0:T(8,128)(2,1)} %param.15) | copy-start | bytes 589828
  21.8 9.8 %all-to-all-start = ((bf16[4,2,12288]{2,1,0:T(2,128)(2,1)}), bf16[4,2,12288]{2,1,0:T(2,128)(2,1)S(1)}, u32[]{:S(2)}, u32[]{:S(2)}) async-start(bf16[4,2,12288]{2,1,0:T(2,128)(2,1)} %reshape.124), calls=%async_computation | async-start | bytes 393216 | tf_op jit(solution)/shard_map/all_to_all | solution.py:131
  31.6 43.1 %all-to-all-start.2 = ((bf16[4,2,12288]{2,1,0:T(2,128)(2,1)}), bf16[4,2,12288]{2,1,0:T(2,128)(2,1)}, u32[]{:S(2)}, u32[]{:S(2)}) async-start(bf16[4,2,12288]{2,1,0:T(2,128)(2,1)} %reshape.126), calls=%async_computation.2 | async-start | bytes 393216 | tf_op jit(solution)/shard_map/all_to_all | solution.py:133
  35.6 173.3 %reduce-scatter.2.cloned.1.call-start = ((), (), s32[]{:S(2)}) async-start(), calls=%async_computation.5 | async-start | bytes 1638400 | tf_op jit(solution)/shard_map/reduce_scatter | solution.py:164
  118.2 1.2 copy-start.2
  120.5 63.6 %copy-start.9 = (f32[5120]{0:T(1024)S(1)}, f32[5120]{0:T(1024)}, u32[]{:S(2)}) copy-start(f32[5120]{0:T(1024)} %param.20) | copy-start | bytes 61444
  120.5 88.4 %copy-start.10 = (f32[5120]{0:T(1024)S(1)}, f32[5120]{0:T(1024)}, u32[]{:S(2)}) copy-start(f32[5120]{0:T(1024)} %param.18) | copy-start | bytes 61444
  184.1 24.9 %copy-start.4 = (bf16[2,1,16,5120]{3,2,1,0:T(8,128)(2,1)S(1)}, bf16[2,1,16,5120]{3,2,1,0:T(8,128)(2,1)}, u32[]{:S(2)}) copy-start(bf16[2,1,16,5120]{3,2,1,0:T(8,128)(2,1)} %param.16) | copy-start | bytes 983044
  184.1 26.3 %copy-start.8 = (f32[5120]{0:T(1024)S(1)}, f32[5120]{0:T(1024)}, u32[]{:S(2)}) copy-start(f32[5120]{0:T(1024)} %param.19) | copy-start | bytes 61444
  184.1 26.5 %copy-start.13 = (f32[64]{0:T(128)S(1)}, f32[64]{0:T(128)}, u32[]{:S(2)}) copy-start(f32[64]{0:T(128)} %param.22) | copy-start | bytes 772
  210.1 13.1 %copy-start.1 = (bf16[2,1,16,5120]{3,2,0,1:T(8,128)(2,1)}, bf16[2,1,16,5120]{3,2,0,1:T(8,128)(2,1)S(1)}, u32[]{:S(2)}) copy-start(bf16[2,1,16,5120]{3,2,0,1:T(8,128)(2,1)S(1)} %get-tuple-element.36) | copy-start | bytes 983044
  211.0 2.4 %collective-permute-start = (bf16[2,2,32,16]{3,2,1,0:T(8,128)(2,1)S(1)}, bf16[2,2,32,16]{3,2,1,0:T(8,128)(2,1)S(1)}, u32[]{:S(2)}, u32[]{:S(2)}) collective-permute-start(bf16[2,2,32,16]{3,2,1,0:T(8,128)(2,1)S(1)} %bitcast.101), channel_id=1, source_target_pairs={{0,1},{1,2},{2,3},{4,5},{5,6},{6,7},{8,9},{9,10},{10,11},{12,13},{... | collective-permute-start | bytes 12296 | tf_op jit(solution)/shard_map/ppermute | solution.py:12
  213.5 5.0 %collective-permute-start.1 = (bf16[4,1,32,16]{3,2,1,0:T(8,128)(2,1)S(1)}, bf16[4,1,32,16]{3,2,1,0:T(8,128)(2,1)S(1)}, u32[]{:S(2)}, u32[]{:S(2)}) collective-permute-start(bf16[4,1,32,16]{3,2,1,0:T(8,128)(2,1)S(1)} %get-tuple-element.63), channel_id=1, source_target_pairs={{0,4},{4,8},{8,12},{1,5},{5,9},{9,13},{2,6},{6,10},{10,14},{3,7},{... | collective-permute-start | bytes 12296 | tf_op jit(solution)/shard_map/ppermute | solution.py:22
  216.9 6.1 %collective-permute-start.2 = (bf16[4,1,32,16]{3,2,1,0:T(8,128)(2,1)S(1)}, bf16[4,1,32,16]{3,2,1,0:T(8,128)(2,1)S(1)}, u32[]{:S(2)}, u32[]{:S(2)}) collective-permute-start(bf16[4,1,32,16]{3,2,1,0:T(8,128)(2,1)S(1)} %get-tuple-element.64), channel_id=1, source_target_pairs={{4,0},{8,4},{12,8},{5,1},{9,5},{13,9},{6,2},{10,6},{14,10},{7,3},{... | collective-permute-start | bytes 12296 | tf_op jit(solution)/shard_map/ppermute | solution.py:23
  223.0 1.0 copy-start.3
  223.1 1.0 copy-start.11
  223.1 1.3 copy-start.12
Sparse Core Ops, SparseCore 0:
  9.6 168.8 all-gather.1
  184.2 24.6 reduce-scatter.1
where the time goes:
time: 233 us; the launch traced here: 232 us
  waiting for transfers between devices  90.3 us (39%)
  blocking collectives  68.1 us (29%)
  local copies, waits for them, and re-layouts  30.9 us (13%)
  starting transfers between devices  18 us (8%)
  between operations  14.5 us (6%)
  matrix products  7.28 us (3%)
  other arithmetic  3.08 us (1%)
    all_gather x1, waiting for transfers between devices, on_device(): lax.all_gather(out_weight, 'seq', axis=1, tiled=True)  57.9 us
    all_gather x1, blocking collectives, on_device(): lax.all_gather(local_keys, 'seq', axis=1, tiled=True)  35.5 us
    all_gather x1, blocking collectives, on_device(): lax.all_gather(local_values, 'seq', axis=1, tiled=True)  32.6 us
    reduce_scatter x1, waiting for transfers between devices, on_device(): lax.psum_scatter(partial_value.astype(jnp.bfloat16), 'head', scatter_dime...  24.8 us
    unnamed x37, local copies, waits for them, and re-layouts  21.1 us
    dot_general x1, matrix products, on_device(): jnp.dot(attended, lax.all_gather(out_weight, 'seq', axis=1, tiled=True),...  5.58 us
  transfers between devices with their start and end apart: 8, of which 6 were waited for; matrix products, arithmetic and copies ran while one was open for 13% of the time, Pallas kernels for 0%

commit v1 on v0

--- a/solution.py
+++ b/solution.py
@@ -1,6 +1,8 @@
 import jax
 import jax.numpy as jnp
 from jax import lax
+from jax.experimental import pallas as pl
+from jax.experimental.pallas import tpu as pltpu
 from jax.sharding import PartitionSpec as P
 
 HEAD_DIM = 128
@@ -107,7 +109,7 @@
     return carried
 
 
-def on_device(
+def general_path(
     queries,
     attn_keys,
     attn_values,
@@ -174,6 +176,287 @@
     return (hidden, features)
 
 
+def pack_heads(queries, keys, values, seq_count, head_count):
+    tokens, width = queries.shape
+    group = width // HEAD_DIM // head_count
+    whole, shared = divmod(group, seq_count)
+    slots = whole + (shared > 0)
+
+    def heads_of(seq):
+        owned = [seq * whole + i for i in range(whole)]
+        if shared:
+            owned.append(whole * seq_count + seq // (seq_count // shared))
+        return owned
+
+    def kernel(q_ref, k_ref, v_ref, out_ref):
+        for seq in range(seq_count):
+            for head in range(head_count):
+                for slot, local in enumerate(heads_of(seq)):
+                    col = (head * group + local) * HEAD_DIM
+                    for part, ref in enumerate((q_ref, k_ref, v_ref)):
+                        to = (slot * 3 + part) * HEAD_DIM
+                        out_ref[seq * head_count + head, :, to : to + HEAD_DIM] = ref[
+                            :, col : col + HEAD_DIM
+                        ]
+
+    return pl.pallas_call(
+        kernel,
+        out_shape=jax.ShapeDtypeStruct(
+            (seq_count * head_count, tokens, slots * 3 * HEAD_DIM), queries.dtype
+        ),
+        name="pack_heads",
+    )(queries, keys, values)
+
+
+def attend_kernel_call(packed, seq_count, head_count, group):
+    tokens = packed.shape[1]
+    whole, shared = divmod(group, seq_count)
+    sharers = seq_count // shared if shared else 1
+    row = head_count * tokens
+    total = seq_count * row
+    part_rows = seq_count // sharers
+    out_blocks = whole * seq_count + (part_rows if shared else 0)
+    part = (lax.axis_index("seq") % sharers).astype(jnp.int32).reshape(1)
+
+    def kernel(part_ref, x_ref, out_ref):
+        def one(slot, first, rows_of_seq, base):
+            at = slot * 3 * HEAD_DIM
+            count = rows_of_seq * head_count
+            q = x_ref[pl.ds(first, count), :, at : at + HEAD_DIM]
+            q = q.reshape(count * tokens, HEAD_DIM)
+            k = x_ref[:, :, at + HEAD_DIM : at + 2 * HEAD_DIM].reshape(total, HEAD_DIM)
+            v = x_ref[:, :, at + 2 * HEAD_DIM : at + 3 * HEAD_DIM].reshape(total, HEAD_DIM)
+            scores = lax.dot_general(
+                q, k, (((1,), (1,)), ((), ())), preferred_element_type=jnp.float32
+            )
+            scores = scores * HEAD_DIM ** (-0.5)
+            weights = jnp.exp(scores - jnp.max(scores, -1, keepdims=True))
+            denominator = jnp.sum(weights, -1, keepdims=True)
+            product = jnp.dot(weights.astype(jnp.bfloat16), v, preferred_element_type=jnp.float32)
+            result = (product / denominator).astype(jnp.bfloat16)
+            for seq in range(rows_of_seq):
+                for head in range(head_count):
+                    at_row = (seq * head_count + head) * tokens
+                    to = (base + seq) * tokens
+                    out_ref[head, to : to + tokens, :] = result[at_row : at_row + tokens, :]
+
+        for slot in range(whole):
+            one(slot, 0, seq_count, slot * seq_count)
+        if shared:
+            one(whole, part_ref[0] * part_rows * head_count, part_rows, whole * seq_count)
+
+    return pl.pallas_call(
+        kernel,
+        in_specs=[
+            pl.BlockSpec(memory_space=pltpu.SMEM),
+            pl.BlockSpec(memory_space=pltpu.VMEM),
+        ],
+        out_shape=jax.ShapeDtypeStruct(
+            (head_count, out_blocks * tokens, HEAD_DIM), jnp.bfloat16
+        ),
+        name="attend",
+    )(part, packed)
+
+
+def project_kernel_call(gathered, weights, seq_count, head_count, group, tokens):
+    whole, shared = divmod(group, seq_count)
+    sharers = seq_count // shared if shared else 1
+    part_rows = seq_count // sharers
+    rows = seq_count * tokens
+    width = weights[0].shape[1]
+    block = width // 5 if width % 640 == 0 else width
+    me = lax.axis_index("head").astype(jnp.int32).reshape(1)
+
+    def kernel(me_ref, x_ref, *refs):
+        w_refs, out_ref, a_ref = (refs[:-2], refs[-2], refs[-1])
+
+        @pl.when(pl.program_id(0) == 0)
+        def _():
+            for seq in range(seq_count):
+                for head in range(head_count):
+                    for slot in range(whole):
+                        col = (seq * whole + slot) * HEAD_DIM
+                        a_ref[head, :, col : col + HEAD_DIM] = x_ref[
+                            seq, head, slot * rows : (slot + 1) * rows, :
+                        ]
+                    if shared:
+                        col = (whole * seq_count + seq // sharers) * HEAD_DIM
+                        to = (seq % sharers) * part_rows * tokens
+                        a_ref[head, to : to + part_rows * tokens, col : col + HEAD_DIM] = x_ref[
+                            seq, head, whole * rows : whole * rows + part_rows * tokens, :
+                        ]
+
+        total = None
+        for offset, w_ref in enumerate(w_refs):
+            term = jnp.dot(
+                a_ref[me_ref[0] ^ offset], w_ref[...], preferred_element_type=jnp.float32
+            )
+            total = term if total is None else total + term
+        total = total.astype(jnp.bfloat16)
+        for seq in range(seq_count):
+            out_ref[seq] = total[seq * tokens : (seq + 1) * tokens]
+
+    return pl.pallas_call(
+        kernel,
+        grid=(width // block,),
+        in_specs=[
+            pl.BlockSpec(memory_space=pltpu.SMEM),
+            pl.BlockSpec(gathered.shape, lambda i: (0, 0, 0, 0)),
+        ]
+        + [pl.BlockSpec((w.shape[0], block), lambda i: (0, i)) for w in weights],
+        out_specs=pl.BlockSpec((seq_count, tokens, block), lambda i: (0, 0, i)),
+        out_shape=jax.ShapeDtypeStruct((seq_count, tokens, width), jnp.bfloat16),
+        scratch_shapes=[pltpu.VMEM((head_count, rows, group * HEAD_DIM), jnp.bfloat16)],
+        name="project",
+    )(me, gathered, *weights)
+
+
+def finish_kernel_call(columns, residual, gate, shift, scale, head_weight, head_bias):
+    parts, tokens, width = columns.shape
+    model = parts * width
+
+    def kernel(y_ref, r_ref, g_ref, sh_ref, sc_ref, w_ref, b_ref, h_ref, p_ref):
+        total = jnp.zeros((tokens, 1), jnp.float32)
+        for i in range(parts):
+            at = slice(i * width, (i + 1) * width)
+            hidden = (
+                r_ref[:, at].astype(jnp.float32) + g_ref[:, at] * y_ref[i].astype(jnp.float32)
+            ).astype(jnp.bfloat16)
+            h_ref[:, at] = hidden
+            total = total + jnp.sum(hidden.astype(jnp.float32), -1, keepdims=True)
+        mean = total / model
+        square = jnp.zeros((tokens, 1), jnp.float32)
+        for i in range(parts):
+            center = h_ref[:, i * width : (i + 1) * width].astype(jnp.float32) - mean
+            square = square + jnp.sum(center * center, -1, keepdims=True)
+        inverse = lax.rsqrt(square / model + 1e-06)
+        latent = jnp.zeros((tokens, w_ref.shape[1]), jnp.float32)
+        for i in range(parts):
+            at = slice(i * width, (i + 1) * width)
+            center = h_ref[:, at].astype(jnp.float32) - mean
+            normed = (center * inverse * (1.0 + sc_ref[:, at]) + sh_ref[:, at]).astype(jnp.bfloat16)
+            latent = latent + jnp.dot(normed, w_ref[at, :], preferred_element_type=jnp.float32)
+        p_ref[...] = (latent + b_ref[...]).astype(jnp.bfloat16)
+
+    return pl.pallas_call(
+        kernel,
+        out_shape=(
+            jax.ShapeDtypeStruct((tokens, model), jnp.bfloat16),
+            jax.ShapeDtypeStruct((tokens, head_weight.shape[1]), jnp.bfloat16),
+        ),
+        name="finish",
+    )(
+        columns,
+        residual,
+        gate.reshape(1, -1),
+        shift.reshape(1, -1),
+        scale.reshape(1, -1),
+        head_weight,
+        head_bias.reshape(1, -1),
+    )
+
+
+def neighbour(value, seq_step, head_step):
+    seq_count, head_count = (lax.axis_size("seq"), lax.axis_size("head"))
+    pairs = []
+    for seq in range(seq_count):
+        for head in range(head_count):
+            to_seq, to_head = (seq + seq_step, head + head_step)
+            if 0 <= to_seq < seq_count and 0 <= to_head < head_count:
+                pairs.append((seq * head_count + head, to_seq * head_count + to_head))
+    return lax.ppermute(value, ("seq", "head"), pairs)
+
+
+def all_groups(weight, head_count):
+    held = {0: weight}
+    bit = head_count // 2
+    while bit:
+        pairs = [(i, i ^ bit) for i in range(head_count)]
+        held.update({j ^ bit: lax.ppermute(w, "head", pairs) for j, w in list(held.items())})
+        bit //= 2
+    return [held[j] for j in range(head_count)]
+
+
+def on_device(
+    queries,
+    attn_keys,
+    attn_values,
+    residual,
+    out_weight,
+    out_gate,
+    head_shift,
+    head_scale,
+    head_weight,
+    head_bias,
+    conv_weight,
+    conv_bias,
+    norm_gain,
+):
+    head_count, seq_count = (lax.axis_size("head"), lax.axis_size("seq"))
+    frames, height, breadth, width = queries.shape
+    group = width // HEAD_DIM // head_count
+    shared = group % seq_count
+    tokens = frames * height * breadth
+    fits = (
+        group >= seq_count
+        and (shared == 0 or seq_count % shared == 0)
+        and head_count & (head_count - 1) == 0
+        and height == 1
+        and tokens % 16 == 0
+        and frames >= 2
+    )
+    if not fits:
+        return general_path(
+            queries,
+            attn_keys,
+            attn_values,
+            residual,
+            out_weight,
+            out_gate,
+            head_shift,
+            head_scale,
+            head_weight,
+            head_bias,
+            conv_weight,
+            conv_bias,
+            norm_gain,
+        )
+    weights = all_groups(out_weight, head_count)
+    packed = pack_heads(
+        queries.reshape(tokens, width),
+        attn_keys.reshape(tokens, width),
+        attn_values.reshape(tokens, width),
+        seq_count,
+        head_count,
+    )
+    packed = lax.all_to_all(packed, ("seq", "head"), split_axis=0, concat_axis=0, tiled=True)
+    attended = attend_kernel_call(packed, seq_count, head_count, group)
+    attended = lax.all_to_all(attended, "head", split_axis=0, concat_axis=0, tiled=True)
+    gathered = lax.all_gather(attended, "seq", axis=0, tiled=False)
+    columns = project_kernel_call(gathered, weights, seq_count, head_count, group, tokens)
+    columns = lax.all_to_all(columns, "seq", split_axis=0, concat_axis=0, tiled=True)
+    hidden, latent = finish_kernel_call(
+        columns,
+        residual.reshape(tokens, -1),
+        out_gate,
+        head_shift,
+        head_scale,
+        head_weight,
+        head_bias,
+    )
+    before = [neighbour(latent, step, 1) for step in (1, 0, -1)]
+    now = [neighbour(latent, 1, 0), latent, neighbour(latent, -1, 0)]
+    channels = latent.shape[1] // 4
+    grid = jnp.stack([jnp.stack(before), jnp.stack(now)]).reshape(
+        2, 3, frames, breadth, 2, 2, channels
+    )
+    video = grid.transpose(0, 2, 1, 4, 3, 5, 6).reshape(2 * frames, 6, 2 * breadth, channels)
+    video = video[frames - 2 :, 1:5]
+    padded = jnp.pad(video, ((0, 0), (0, 0), (1, 1), (0, 0)))
+    features = convolve(padded, frames, conv_weight, conv_bias, norm_gain)
+    return (hidden.reshape(residual.shape), features)
+
+
 def solution(mesh):
     return jax.shard_map(
         on_device,

time: 233 us -> 147 us (0.63)
  blocking collectives: 68.1 us -> 19.5 us
  local copies, waits for them, and re-layouts: 30.9 us -> 4.94 us
  Pallas kernels: 0 us -> 14.9 us
  waiting for transfers between devices: 90.3 us -> 76.1 us
  between operations: 14.5 us -> 0.86 us
  starting transfers between devices: 18 us -> 28.3 us
  matrix products: 7.28 us -> 0.31 us
    all_gather x1 -> x0, waiting for transfers between devices: 57.9 us -> none  [on_device(): lax.all_gather(out_weight, 'seq', axis=1, tiled=True)]
    all_gather x2 -> x1, blocking collectives: 68.1 us -> 19.5 us  [on_device(): gathered = lax.all_gather(attended, 'seq', axis=0, tiled=False)]
    ppermute x3 -> x8, waiting for transfers between devices: 5.6 us -> 46.3 us  [the longest x3 43 us: all_groups(): lax.ppermute(w, 'head', pairs)]
    all_to_all x3, waiting for transfers between devices: 1.19 us -> 29.8 us  [the longest x1 18.7 us: on_device(): lax.all_to_all(packed, ('seq', 'head'), split_axis=0, concat_axis=0, tile...]
    reduce_scatter x1 -> x0, waiting for transfers between devices: 24.8 us -> none  [on_device(): lax.psum_scatter(partial_value.astype(jnp.bfloat16), 'head', scatter_dime...]
    unnamed x37 -> x15, local copies, waits for them, and re-layouts: 21.1 us -> 3.05 us
    pallas_call x0 -> x4, Pallas kernels: none -> 14.9 us  [the longest x1 6.69 us: project_kernel_call(): pl.pallas_call(kernel, grid=(width // block,), in_specs=[pl.BlockSpec(mem...]
    ppermute x3 -> x8, starting transfers between devices: 6.26 us -> 15.3 us  [the longest x5 12.3 us: neighbour(): return lax.ppermute(value, ('seq', 'head'), pairs)]
  transfers between devices with their start and end apart: 8 -> 11, of which waited for: 6 -> 5; matrix products, arithmetic and copies ran while one was open for 13% -> 2% of each run, Pallas kernels for 0% -> 4%
where the time goes in v1:
time: 147 us; the launch traced here: 146 us
  waiting for transfers between devices  76.1 us (52%)
  starting transfers between devices  28.3 us (19%)
  blocking collectives  19.5 us (13%)
  Pallas kernels  14.9 us (10%)
  local copies, waits for them, and re-layouts  4.94 us (3%)
    ppermute x3, waiting for transfers between devices, all_groups(): lax.ppermute(w, 'head', pairs)  43 us
    all_gather x1, blocking collectives, on_device(): gathered = lax.all_gather(attended, 'seq', axis=0, tiled=False)  19.5 us
    all_to_all x1, waiting for transfers between devices, on_device(): lax.all_to_all(packed, ('seq', 'head'), split_axis=0, concat_axis=0, tile...  18.7 us
    ppermute x5, starting transfers between devices, neighbour(): return lax.ppermute(value, ('seq', 'head'), pairs)  12.3 us
    pallas_call x1, Pallas kernels, project_kernel_call(): pl.pallas_call(kernel, grid=(width // block,), in_specs=[pl.BlockSpec(mem...  6.69 us
    all_to_all x1, starting transfers between devices, on_device(): lax.all_to_all(packed, ('seq', 'head'), split_axis=0, concat_axis=0, tile...  6.16 us
    all_to_all x1, waiting for transfers between devices, on_device(): lax.all_to_all(columns, 'seq', split_axis=0, concat_axis=0, tiled=True)  5.85 us
    all_to_all x1, waiting for transfers between devices, on_device(): lax.all_to_all(attended, 'head', split_axis=0, concat_axis=0, tiled=True)  5.27 us
  transfers between devices with their start and end apart: 11, of which 5 were waited for; matrix products, arithmetic and copies ran while one was open for 2% of the time, Pallas kernels for 4%

profile of v1, /device:TPU:0, one launch (start us, length us, event | category | flops | bytes accessed | tf_op | source)
XLA Modules:
  0.0 146.1 jit_solution(18220183151441542517)
XLA Ops:
  0.6 0.0 copy-start
  0.6 3.0 %collective-permute-start.1 = (bf16[768,1280]{1,0:T(8,128)(2,1)}, bf16[768,1280]{1,0:T(8,128)(2,1)S(1)}, u32[]{:S(2)}, u32[]{:S(2)}) collective-permute-start(bf16[768,1280]{1,0:T(8,128)(2,1)} %refs_0_.1), channel_id=1, source_target_pairs={{0,2},{1,3},{2,0},{3,1},{4,6},{5,7},{6,4},{7,5},{8,10},{9,11},{10,... | collective-permute-start | bytes 5898248 | tf_op jit(solution)/shard_map/ppermute | solution.py:375
  3.7 0.0 collective-permute-start
  3.7 43.0 %collective-permute-done.1.refs_2_ = bf16[768,1280]{1,0:T(8,128)(2,1)S(1)} collective-permute-done((bf16[768,1280]{1,0:T(8,128)(2,1)}, bf16[768,1280]{1,0:T(8,128)(2,1)S(1)}, u32[]{:S(2)}, u32[]{:S(2)}) %collective-permute-start.1) | collective-permute-done | bytes 1966112 | tf_op jit(solution)/shard_map/ppermute | solution.py:375
  46.7 0.0 copy-start.2
  46.7 0.0 collective-permute-start.2
  46.7 2.8 %pack_heads.1 = bf16[16,32,768]{2,1,0:T(8,128)(2,1)} custom-call(bf16[32,3072]{1,0:T(8,128)(2,1)} %bitcast.28, bf16[32,3072]{1,0:T(8,128)(2,1)} %bitcast.29, bf16[32,3072]{1,0:T(8,128)(2,1)} %bitcast.30), custom_call_target="tpu_custom_call" | custom-call | tf_op jit(solution)/shard_map/pack_heads/pallas_call | solution.py:202
  49.5 6.2 %all-to-all-start = ((bf16[16,32,768]{2,1,0:T(8,128)(2,1)}), bf16[16,32,768]{2,1,0:T(8,128)(2,1)S(1)}, u32[]{:S(2)}, u32[]{:S(2)}) async-start(bf16[16,32,768]{2,1,0:T(8,128)(2,1)} %pack_heads.1), calls=%async_computation | async-start | bytes 1572864 | tf_op jit(solution)/shard_map/all_to_all | solution.py:432
  55.7 18.7 %all-to-all-done.x_ref = bf16[16,32,768]{2,1,0:T(8,128)(2,1)S(1)} async-done(((bf16[16,32,768]{2,1,0:T(8,128)(2,1)}), bf16[16,32,768]{2,1,0:T(8,128)(2,1)S(1)}, u32[]{:S(2)}, u32[]{:S(2)}) %all-to-all-start) | async-done | bytes 786464 | tf_op jit(solution)/shard_map/all_to_all | solution.py:432
  74.4 0.0 copy-start.1
  74.4 0.9 copy-done.1
  75.2 2.6 %attend.1 = bf16[4,192,128]{2,1,0:T(8,128)(2,1)} custom-call(s32[1]{0:T(128)} %bitcast.1.part_ref, bf16[16,32,768]{2,1,0:T(8,128)(2,1)} %copy-done.1), custom_call_target="tpu_custom_call" | custom-call | tf_op jit(solution)/shard_map/attend/pallas_call | solution.py:248
  77.9 0.0 copy-done.2
  77.9 3.4 %all-to-all-start.1 = ((bf16[4,192,128]{2,1,0:T(8,128)(2,1)}), bf16[4,192,128]{2,1,0:T(8,128)(2,1)S(1)}, u32[]{:S(2)}, u32[]{:S(2)}) async-start(bf16[4,192,128]{2,1,0:T(8,128)(2,1)} %attend.1), calls=%async_computation.1 | async-start | bytes 393216 | tf_op jit(solution)/shard_map/all_to_all | solution.py:434
  81.2 5.3 %all-to-all-done.1 = bf16[4,192,128]{2,1,0:T(8,128)(2,1)S(1)} async-done(((bf16[4,192,128]{2,1,0:T(8,128)(2,1)}), bf16[4,192,128]{2,1,0:T(8,128)(2,1)S(1)}, u32[]{:S(2)}, u32[]{:S(2)}) %all-to-all-start.1) | async-done | bytes 196640 | tf_op jit(solution)/shard_map/all_to_all | solution.py:434
  86.5 19.5 %all-gather = bf16[16,192,128]{2,1,0:T(8,128)(2,1)} all-gather(bf16[4,192,128]{2,1,0:T(8,128)(2,1)S(1)} %all-to-all-done.1), channel_id=2, replica_groups=mesh['clip'=2,'seq'=4,'head'=4] {'seq'}, dimensions={0}, use_global_device_ids=true | all-gather | bytes 983040 | tf_op jit(solution)/shard_map/all_gather | solution.py:435
  106.0 0.0 collective-permute-done.refs_1_
  106.0 0.0 collective-permute-done.2.refs_3_
  106.0 0.0 copy-start.4
  106.0 6.7 %project.1 = bf16[4,32,1280]{2,1,0:T(8,128)(2,1)} custom-call(s32[1]{0:T(128)} %bitcast.me_ref, bf16[4,4,192,128]{3,2,1,0:T(8,128)(2,1)} %bitcast.23, bf16[768,1280]{1,0:T(8,128)(2,1)} %refs_0_.1, bf16[768,1280]{1,0:T(8,128)(2,1)} %collective-permute-done.refs_1_, bf16[768,1280]{1,0:T(8,128)(2,1)} %copy-done.2, bf16[768,1280]{1,0:T(8,128)(2,1)} %collective-permute-done.2.refs_3_), custom_call_target="tpu_custom_call" | custom-call | tf_op jit(solution)/shard_map/project/pallas_call | solution.py:299
  112.7 3.5 %all-to-all-start.2 = ((bf16[4,32,1280]{2,1,0:T(8,128)(2,1)}), bf16[4,32,1280]{2,1,0:T(8,128)(2,1)S(1)}, u32[]{:S(2)}, u32[]{:S(2)}) async-start(bf16[4,32,1280]{2,1,0:T(8,128)(2,1)} %project.1), calls=%async_computation.2 | async-start | bytes 655360 | tf_op jit(solution)/shard_map/all_to_all | solution.py:437
  116.2 0.0 copy-done.4
  116.2 1.4 copy.25.w_ref
  117.6 5.8 %all-to-all-done.2.y_ref = bf16[4,32,1280]{2,1,0:T(8,128)(2,1)S(1)} async-done(((bf16[4,32,1280]{2,1,0:T(8,128)(2,1)}), bf16[4,32,1280]{2,1,0:T(8,128)(2,1)S(1)}, u32[]{:S(2)}, u32[]{:S(2)}) %all-to-all-start.2) | async-done | bytes 327712 | tf_op jit(solution)/shard_map/all_to_all | solution.py:437
  123.4 0.0 copy-start.3
  123.4 0.7 copy-done.3
  124.2 2.8 %finish.1 = (bf16[32,5120]{1,0:T(8,128)(2,1)}, bf16[32,64]{1,0:T(8,128)(2,1)}) custom-call(bf16[4,32,1280]{2,1,0:T(8,128)(2,1)} %copy-done.3, bf16[32,5120]{1,0:T(8,128)(2,1)} %bitcast.27, f32[1,5120]{1,0:T(1,128)} %bitcast.32, f32[1,5120]{1,0:T(1,128)} %bitcast.33, f32[1,5120]{1,0:T(1,128)} %bitcast.34, bf16[5120,64]{1,0:T(8,128)(2,1)} %copy.25.w_ref, ...), custom_call_target="tpu_custom_call" | custom-call | tf_op jit(solution)/shard_map/finish/pallas_call | solution.py:341
  126.9 0.0 copy-start.5
  126.9 1.4 collective-permute-start.3
  128.3 4.1 %collective-permute-start.4 = (bf16[32,64]{1,0:T(8,128)(2,1)}, bf16[32,64]{1,0:T(8,128)(2,1)S(1)}, u32[]{:S(2)}, u32[]{:S(2)}) collective-permute-start(bf16[32,64]{1,0:T(8,128)(2,1)} %get-tuple-element.5), channel_id=1, source_target_pairs={{0,1},{1,2},{2,3},{4,5},{5,6},{6,7},{8,9},{9,10},{10,11},{12,13},{... | collective-permute-start | bytes 12296 | tf_op jit(solution)/shard_map/ppermute | solution.py:367
  132.5 0.7 collective-permute-start.5
  133.1 4.8 %collective-permute-start.6 = (bf16[32,64]{1,0:T(8,128)(2,1)}, bf16[32,64]{1,0:T(8,128)(2,1)S(1)}, u32[]{:S(2)}, u32[]{:S(2)}) collective-permute-start(bf16[32,64]{1,0:T(8,128)(2,1)} %get-tuple-element.5), channel_id=1, source_target_pairs={{0,4},{1,5},{2,6},{3,7},{4,8},{5,9},{6,10},{7,11},{8,12},{9,13},{1... | collective-permute-start | bytes 12296 | tf_op jit(solution)/shard_map/ppermute | solution.py:367
  137.9 1.3 collective-permute-start.7
  139.2 0.8 stack.34
  140.0 0.0 collective-permute-done.3
  140.0 0.1 stack.29
  140.1 0.0 collective-permute-done.4
  140.1 0.1 stack.30
  140.2 0.0 collective-permute-done.5
  140.2 0.1 stack.31
  140.3 0.0 collective-permute-done.6
  140.3 0.1 stack.33
  140.4 3.3 %collective-permute-done.7 = bf16[32,64]{1,0:T(8,128)(2,1)S(1)} collective-permute-done((bf16[32,64]{1,0:T(8,128)(2,1)}, bf16[32,64]{1,0:T(8,128)(2,1)S(1)}, u32[]{:S(2)}, u32[]{:S(2)}) %collective-permute-start.7) | collective-permute-done | bytes 4128 | tf_op jit(solution)/shard_map/ppermute | solution.py:367
  143.7 0.1 stack.35
  143.8 0.0 copy-start.6
  143.8 0.4 maximum_maximum_fusion
  144.2 0.2 copy.35
  144.4 0.1 pad_slice_fusion
  144.6 0.3 concatenate.6
  144.9 0.0 copy-done
  145.0 0.0 copy-done.5
  145.0 0.3 multiply_reduce_fusion
  145.3 0.0 copy-done.6
  145.3 0.8 multiply_convert_fusion
  (3 shorter events, 0.1 us)
Async XLA Ops:
  0.6 144.3 %copy-start = (bf16[3,3,3,16,384]{4,3,2,1,0:T(8,128)(2,1)S(1)}, bf16[3,3,3,16,384]{4,3,2,1,0:T(8,128)(2,1)}, u32[]{:S(2)}) copy-start(bf16[3,3,3,16,384]{4,3,2,1,0:T(8,128)(2,1)} %param.23) | copy-start | bytes 995332
  0.6 46.1 %collective-permute-start.1 = (bf16[768,1280]{1,0:T(8,128)(2,1)}, bf16[768,1280]{1,0:T(8,128)(2,1)S(1)}, u32[]{:S(2)}, u32[]{:S(2)}) collective-permute-start(bf16[768,1280]{1,0:T(8,128)(2,1)} %refs_0_.1), channel_id=1, source_target_pairs={{0,2},{1,3},{2,0},{3,1},{4,6},{5,7},{6,4},{7,5},{8,10},{9,11},{10,... | collective-permute-start | bytes 5898248 | tf_op jit(solution)/shard_map/ppermute | solution.py:375
  3.7 102.3 %collective-permute-start = (bf16[768,1280]{1,0:T(8,128)(2,1)}, bf16[768,1280]{1,0:T(8,128)(2,1)}, u32[]{:S(2)}, u32[]{:S(2)}) collective-permute-start(bf16[768,1280]{1,0:T(8,128)(2,1)} %refs_0_.1), channel_id=1, source_target_pairs={{0,1},{1,0},{2,3},{3,2},{4,5},{5,4},{6,7},{7,6},{8,9},{9,8},{10,11... | collective-permute-start | bytes 5898248 | tf_op jit(solution)/shard_map/ppermute | solution.py:375
  46.7 31.1 %copy-start.2 = (bf16[768,1280]{1,0:T(8,128)(2,1)}, bf16[768,1280]{1,0:T(8,128)(2,1)S(1)}, u32[]{:S(2)}) copy-start(bf16[768,1280]{1,0:T(8,128)(2,1)S(1)} %collective-permute-done.1.refs_2_) | copy-start | bytes 5898244
  46.7 59.3 %collective-permute-start.2 = (bf16[768,1280]{1,0:T(8,128)(2,1)S(1)}, bf16[768,1280]{1,0:T(8,128)(2,1)}, u32[]{:S(2)}, u32[]{:S(2)}) collective-permute-start(bf16[768,1280]{1,0:T(8,128)(2,1)S(1)} %collective-permute-done.1.refs_2_), channel_id=1, source_target_pairs={{0,1},{1,0},{2,3},{3,2},{4,5},{5,4},{6,7},{7,6},{8,9},{9,8},{10,11... | collective-permute-start | bytes 5898248 | tf_op jit(solution)/shard_map/ppermute | solution.py:375
  49.5 24.8 %all-to-all-start = ((bf16[16,32,768]{2,1,0:T(8,128)(2,1)}), bf16[16,32,768]{2,1,0:T(8,128)(2,1)S(1)}, u32[]{:S(2)}, u32[]{:S(2)}) async-start(bf16[16,32,768]{2,1,0:T(8,128)(2,1)} %pack_heads.1), calls=%async_computation | async-start | bytes 1572864 | tf_op jit(solution)/shard_map/all_to_all | solution.py:432
  74.4 0.9 copy-start.1
  77.9 8.6 %all-to-all-start.1 = ((bf16[4,192,128]{2,1,0:T(8,128)(2,1)}), bf16[4,192,128]{2,1,0:T(8,128)(2,1)S(1)}, u32[]{:S(2)}, u32[]{:S(2)}) async-start(bf16[4,192,128]{2,1,0:T(8,128)(2,1)} %attend.1), calls=%async_computation.1 | async-start | bytes 393216 | tf_op jit(solution)/shard_map/all_to_all | solution.py:434
  106.0 10.2 %copy-start.4 = (bf16[5120,64]{0,1:T(8,128)(2,1)S(1)}, bf16[5120,64]{0,1:T(8,128)(2,1)}, u32[]{:S(2)}) copy-start(bf16[5120,64]{0,1:T(8,128)(2,1)} %param.21) | copy-start | bytes 1966084
  112.7 10.7 %all-to-all-start.2 = ((bf16[4,32,1280]{2,1,0:T(8,128)(2,1)}), bf16[4,32,1280]{2,1,0:T(8,128)(2,1)S(1)}, u32[]{:S(2)}, u32[]{:S(2)}) async-start(bf16[4,32,1280]{2,1,0:T(8,128)(2,1)} %project.1), calls=%async_computation.2 | async-start | bytes 655360 | tf_op jit(solution)/shard_map/all_to_all | solution.py:437
  123.4 0.7 copy-start.3
  126.9 18.0 %copy-start.5 = (f32[384]{0:T(512)S(1)}, f32[384]{0:T(512)}, u32[]{:S(2)}) copy-start(f32[384]{0:T(512)} %param.24) | copy-start | bytes 4612
  126.9 13.1 %collective-permute-start.3 = (bf16[32,64]{1,0:T(8,128)(2,1)}, bf16[32,64]{1,0:T(8,128)(2,1)S(1)}, u32[]{:S(2)}, u32[]{:S(2)}) collective-permute-start(bf16[32,64]{1,0:T(8,128)(2,1)} %get-tuple-element.5), channel_id=1, source_target_pairs={{0,5},{1,6},{2,7},{4,9},{5,10},{6,11},{8,13},{9,14},{10,15},{16,21... | collective-permute-start | bytes 12296 | tf_op jit(solution)/shard_map/ppermute | solution.py:367
  128.3 11.8 %collective-permute-start.4 = (bf16[32,64]{1,0:T(8,128)(2,1)}, bf16[32,64]{1,0:T(8,128)(2,1)S(1)}, u32[]{:S(2)}, u32[]{:S(2)}) collective-permute-start(bf16[32,64]{1,0:T(8,128)(2,1)} %get-tuple-element.5), channel_id=1, source_target_pairs={{0,1},{1,2},{2,3},{4,5},{5,6},{6,7},{8,9},{9,10},{10,11},{12,13},{... | collective-permute-start | bytes 12296 | tf_op jit(solution)/shard_map/ppermute | solution.py:367
  132.5 7.7 %collective-permute-start.5 = (bf16[32,64]{1,0:T(8,128)(2,1)}, bf16[32,64]{1,0:T(8,128)(2,1)S(1)}, u32[]{:S(2)}, u32[]{:S(2)}) collective-permute-start(bf16[32,64]{1,0:T(8,128)(2,1)} %get-tuple-element.5), channel_id=1, source_target_pairs={{4,1},{5,2},{6,3},{8,5},{9,6},{10,7},{12,9},{13,10},{14,11},{20,17... | collective-permute-start | bytes 12296 | tf_op jit(solution)/shard_map/ppermute | solution.py:367
  133.1 7.2 %collective-permute-start.6 = (bf16[32,64]{1,0:T(8,128)(2,1)}, bf16[32,64]{1,0:T(8,128)(2,1)S(1)}, u32[]{:S(2)}, u32[]{:S(2)}) collective-permute-start(bf16[32,64]{1,0:T(8,128)(2,1)} %get-tuple-element.5), channel_id=1, source_target_pairs={{0,4},{1,5},{2,6},{3,7},{4,8},{5,9},{6,10},{7,11},{8,12},{9,13},{1... | collective-permute-start | bytes 12296 | tf_op jit(solution)/shard_map/ppermute | solution.py:367
  137.9 5.8 %collective-permute-start.7 = (bf16[32,64]{1,0:T(8,128)(2,1)}, bf16[32,64]{1,0:T(8,128)(2,1)S(1)}, u32[]{:S(2)}, u32[]{:S(2)}) collective-permute-start(bf16[32,64]{1,0:T(8,128)(2,1)} %get-tuple-element.5), channel_id=1, source_target_pairs={{4,0},{5,1},{6,2},{7,3},{8,4},{9,5},{10,6},{11,7},{12,8},{13,9},{1... | collective-permute-start | bytes 12296 | tf_op jit(solution)/shard_map/ppermute | solution.py:367
  143.8 1.5 %copy-start.6 = (f32[384]{0:T(512)S(1)}, f32[384]{0:T(512)}, u32[]{:S(2)}) copy-start(f32[384]{0:T(512)} %param.25) | copy-start | bytes 4612

commit v2 on v1

--- a/solution.py
+++ b/solution.py
@@ -216,9 +216,10 @@
     total = seq_count * row
     part_rows = seq_count // sharers
     out_blocks = whole * seq_count + (part_rows if shared else 0)
-    part = (lax.axis_index("seq") % sharers).astype(jnp.int32).reshape(1)
-
-    def kernel(part_ref, x_ref, out_ref):
+    outer = head_count // 2
+    place = jnp.stack([lax.axis_index("seq") % sharers, lax.axis_index("head") % 2])
+
+    def kernel(place_ref, x_ref, keep_ref, send_ref, result_ref):
         def one(slot, first, rows_of_seq, base):
             at = slot * 3 * HEAD_DIM
             count = rows_of_seq * head_count
@@ -234,79 +235,92 @@
             denominator = jnp.sum(weights, -1, keepdims=True)
             product = jnp.dot(weights.astype(jnp.bfloat16), v, preferred_element_type=jnp.float32)
             result = (product / denominator).astype(jnp.bfloat16)
+            result_ref[0:count] = result.reshape(count, tokens, HEAD_DIM)
             for seq in range(rows_of_seq):
-                for head in range(head_count):
-                    at_row = (seq * head_count + head) * tokens
+                for far in range(outer):
                     to = (base + seq) * tokens
-                    out_ref[head, to : to + tokens, :] = result[at_row : at_row + tokens, :]
+                    mine = seq * head_count + far * 2
+                    keep_ref[far, to : to + tokens, :] = result_ref[mine + place_ref[1]]
+                    send_ref[far, to : to + tokens, :] = result_ref[mine + 1 - place_ref[1]]
 
         for slot in range(whole):
             one(slot, 0, seq_count, slot * seq_count)
         if shared:
-            one(whole, part_ref[0] * part_rows * head_count, part_rows, whole * seq_count)
-
+            one(whole, place_ref[0] * part_rows * head_count, part_rows, whole * seq_count)
+
+    half = jax.ShapeDtypeStruct((outer, out_blocks * tokens, HEAD_DIM), jnp.bfloat16)
     return pl.pallas_call(
         kernel,
         in_specs=[
             pl.BlockSpec(memory_space=pltpu.SMEM),
             pl.BlockSpec(memory_space=pltpu.VMEM),
         ],
-        out_shape=jax.ShapeDtypeStruct(
-            (head_count, out_blocks * tokens, HEAD_DIM), jnp.bfloat16
-        ),
+        out_shape=(half, half),
+        scratch_shapes=[pltpu.VMEM((seq_count * head_count, tokens, HEAD_DIM), jnp.bfloat16)],
         name="attend",
-    )(part, packed)
-
-
-def project_kernel_call(gathered, weights, seq_count, head_count, group, tokens):
+    )(place.astype(jnp.int32), packed)
+
+
+def project_kernel_call(gathered, weights, seq_count, group, tokens):
     whole, shared = divmod(group, seq_count)
     sharers = seq_count // shared if shared else 1
     part_rows = seq_count // sharers
+    outer = gathered.shape[2]
     rows = seq_count * tokens
     width = weights[0].shape[1]
     block = width // 5 if width % 640 == 0 else width
-    me = lax.axis_index("head").astype(jnp.int32).reshape(1)
+    me = (lax.axis_index("head") // 2).astype(jnp.int32).reshape(1)
 
     def kernel(me_ref, x_ref, *refs):
-        w_refs, out_ref, a_ref = (refs[:-2], refs[-2], refs[-1])
+        w_refs = refs[: len(weights)]
+        out_refs = refs[len(weights) : -1]
+        a_ref = refs[-1]
 
         @pl.when(pl.program_id(0) == 0)
         def _():
-            for seq in range(seq_count):
-                for head in range(head_count):
-                    for slot in range(whole):
-                        col = (seq * whole + slot) * HEAD_DIM
-                        a_ref[head, :, col : col + HEAD_DIM] = x_ref[
-                            seq, head, slot * rows : (slot + 1) * rows, :
-                        ]
-                    if shared:
-                        col = (whole * seq_count + seq // sharers) * HEAD_DIM
-                        to = (seq % sharers) * part_rows * tokens
-                        a_ref[head, to : to + part_rows * tokens, col : col + HEAD_DIM] = x_ref[
-                            seq, head, whole * rows : whole * rows + part_rows * tokens, :
-                        ]
+            for step in range(outer):
+                far = (me_ref[0] + step) % outer
+                base = step * rows
+                for seq in range(seq_count):
+                    for near in range(len(weights)):
+                        for slot in range(whole):
+                            col = (seq * whole + slot) * HEAD_DIM
+                            a_ref[near, base : base + rows, col : col + HEAD_DIM] = x_ref[
+                                seq, near, far, slot * rows : (slot + 1) * rows, :
+                            ]
+                        if shared:
+                            col = (whole * seq_count + seq // sharers) * HEAD_DIM
+                            to = base + (seq % sharers) * part_rows * tokens
+                            a_ref[
+                                near, to : to + part_rows * tokens, col : col + HEAD_DIM
+                            ] = x_ref[
+                                seq, near, far, whole * rows : (whole * rows + part_rows * tokens), :
+                            ]
 
         total = None
-        for offset, w_ref in enumerate(w_refs):
-            term = jnp.dot(
-                a_ref[me_ref[0] ^ offset], w_ref[...], preferred_element_type=jnp.float32
-            )
+        for near, w_ref in enumerate(w_refs):
+            term = jnp.dot(a_ref[near], w_ref[...], preferred_element_type=jnp.float32)
             total = term if total is None else total + term
         total = total.astype(jnp.bfloat16)
-        for seq in range(seq_count):
-            out_ref[seq] = total[seq * tokens : (seq + 1) * tokens]
-
+        for step, out_ref in enumerate(out_refs):
+            for seq in range(seq_count):
+                at = step * rows + seq * tokens
+                out_ref[seq] = total[at : at + tokens]
+
+    out = jax.ShapeDtypeStruct((seq_count, tokens, width), jnp.bfloat16)
     return pl.pallas_call(
         kernel,
         grid=(width // block,),
         in_specs=[
             pl.BlockSpec(memory_space=pltpu.SMEM),
-            pl.BlockSpec(gathered.shape, lambda i: (0, 0, 0, 0)),
+            pl.BlockSpec(gathered.shape, lambda i: (0, 0, 0, 0, 0)),
         ]
         + [pl.BlockSpec((w.shape[0], block), lambda i: (0, i)) for w in weights],
-        out_specs=pl.BlockSpec((seq_count, tokens, block), lambda i: (0, 0, i)),
-        out_shape=jax.ShapeDtypeStruct((seq_count, tokens, width), jnp.bfloat16),
-        scratch_shapes=[pltpu.VMEM((head_count, rows, group * HEAD_DIM), jnp.bfloat16)],
+        out_specs=[pl.BlockSpec((seq_count, tokens, block), lambda i: (0, 0, i))] * outer,
+        out_shape=[out] * outer,
+        scratch_shapes=[
+            pltpu.VMEM((len(weights), outer * rows, group * HEAD_DIM), jnp.bfloat16)
+        ],
         name="project",
     )(me, gathered, *weights)
 
@@ -367,14 +381,8 @@
     return lax.ppermute(value, ("seq", "head"), pairs)
 
 
-def all_groups(weight, head_count):
-    held = {0: weight}
-    bit = head_count // 2
-    while bit:
-        pairs = [(i, i ^ bit) for i in range(head_count)]
-        held.update({j ^ bit: lax.ppermute(w, "head", pairs) for j, w in list(held.items())})
-        bit //= 2
-    return [held[j] for j in range(head_count)]
+def swap_near(value, head_count):
+    return lax.ppermute(value, "head", [(i, i ^ 1) for i in range(head_count)])
 
 
 def on_device(
@@ -400,7 +408,7 @@
     fits = (
         group >= seq_count
         and (shared == 0 or seq_count % shared == 0)
-        and head_count & (head_count - 1) == 0
+        and head_count % 2 == 0
         and height == 1
         and tokens % 16 == 0
         and frames >= 2
@@ -421,7 +429,7 @@
             conv_bias,
             norm_gain,
         )
-    weights = all_groups(out_weight, head_count)
+    weights = [out_weight, swap_near(out_weight, head_count)]
     packed = pack_heads(
         queries.reshape(tokens, width),
         attn_keys.reshape(tokens, width),
@@ -430,10 +438,15 @@
         head_count,
     )
     packed = lax.all_to_all(packed, ("seq", "head"), split_axis=0, concat_axis=0, tiled=True)
-    attended = attend_kernel_call(packed, seq_count, head_count, group)
-    attended = lax.all_to_all(attended, "head", split_axis=0, concat_axis=0, tiled=True)
+    keep, send = attend_kernel_call(packed, seq_count, head_count, group)
+    attended = jnp.stack([keep, swap_near(send, head_count)])
     gathered = lax.all_gather(attended, "seq", axis=0, tiled=False)
-    columns = project_kernel_call(gathered, weights, seq_count, head_count, group, tokens)
+    terms = project_kernel_call(gathered, weights, seq_count, group, tokens)
+    columns = terms[0].astype(jnp.float32)
+    for step in range(1, head_count // 2):
+        pairs = [(i, (i + 2 * step) % head_count) for i in range(head_count)]
+        columns = columns + lax.ppermute(terms[step], "head", pairs).astype(jnp.float32)
+    columns = columns.astype(jnp.bfloat16)
     columns = lax.all_to_all(columns, "seq", split_axis=0, concat_axis=0, tiled=True)
     hidden, latent = finish_kernel_call(
         columns,

time: 147 us -> 106 us (0.72)
  waiting for transfers between devices: 76.1 us -> 34.2 us
  other arithmetic: 1.21 us -> 4.56 us
  starting transfers between devices: 28.3 us -> 26.6 us
    ppermute x3, waiting for transfers between devices: 43 us -> 7.5 us  [the longest x1 6.34 us: on_device(): lax.ppermute(terms[step], 'head', pairs).astype(jnp.float32)]
    all_to_all x1 -> x0, waiting for transfers between devices: 5.27 us -> none  [on_device(): lax.all_to_all(attended, 'head', split_axis=0, concat_axis=0, tiled=True)]
    all_to_all x1 -> x0, starting transfers between devices: 3.37 us -> none  [on_device(): lax.all_to_all(attended, 'head', split_axis=0, concat_axis=0, tiled=True)]
    convert_element_type x0 -> x1, other arithmetic: none -> 1.78 us  [on_device(): columns = columns.astype(jnp.bfloat16)]
    another operation x0 -> x2, other arithmetic: none -> 1.57 us  [the longest x1 0.91 us: on_device(): attended = jnp.stack([keep, swap_near(send, head_count)])]
  transfers between devices with their start and end apart: 11 -> 10, of which waited for: 5 -> 5; matrix products, arithmetic and copies ran while one was open for 2% -> 4% of each run, Pallas kernels for 4% -> 3%
where the time goes in v2:
time: 106 us; the launch traced here: 105 us
  waiting for transfers between devices  34.2 us (32%)
  starting transfers between devices  26.6 us (25%)
  blocking collectives  19.9 us (19%)
  Pallas kernels  13.5 us (13%)
  local copies, waits for them, and re-layouts  4.96 us (5%)
  other arithmetic  4.56 us (4%)
    all_gather x1, blocking collectives, on_device(): gathered = lax.all_gather(attended, 'seq', axis=0, tiled=False)  19.9 us
    all_to_all x1, waiting for transfers between devices, on_device(): lax.all_to_all(packed, ('seq', 'head'), split_axis=0, concat_axis=0, tile...  17.5 us
    ppermute x5, starting transfers between devices, neighbour(): return lax.ppermute(value, ('seq', 'head'), pairs)  13.4 us
    all_to_all x1, starting transfers between devices, on_device(): lax.all_to_all(packed, ('seq', 'head'), split_axis=0, concat_axis=0, tile...  7.39 us
    ppermute x1, waiting for transfers between devices, on_device(): lax.ppermute(terms[step], 'head', pairs).astype(jnp.float32)  6.34 us
    all_to_all x1, waiting for transfers between devices, on_device(): lax.all_to_all(columns, 'seq', split_axis=0, concat_axis=0, tiled=True)  5.9 us
    pallas_call x1, Pallas kernels, project_kernel_call(): pl.pallas_call(kernel, grid=(width // block,), in_specs=[pl.BlockSpec(mem...  5.8 us
    all_to_all x1, starting transfers between devices, on_device(): lax.all_to_all(columns, 'seq', split_axis=0, concat_axis=0, tiled=True)  3.55 us
  transfers between devices with their start and end apart: 10, of which 5 were waited for; matrix products, arithmetic and copies ran while one was open for 4% of the time, Pallas kernels for 3%

profile of v2, /device:TPU:0, one launch (start us, length us, event | category | flops | bytes accessed | tf_op | source)
XLA Modules:
  0.0 104.8 jit_solution(9339964580661164125)
XLA Ops:
  0.6 0.0 copy-start
  0.6 0.0 copy-start.2
  0.7 2.3 %pack_heads.1 = bf16[16,32,768]{2,1,0:T(8,128)(2,1)} custom-call(bf16[32,3072]{1,0:T(8,128)(2,1)} %bitcast.31, bf16[32,3072]{1,0:T(8,128)(2,1)} %bitcast.32, bf16[32,3072]{1,0:T(8,128)(2,1)} %bitcast.33), custom_call_target="tpu_custom_call" | custom-call | tf_op jit(solution)/shard_map/pack_heads/pallas_call | solution.py:202
  2.9 7.4 %all-to-all-start = ((bf16[16,32,768]{2,1,0:T(8,128)(2,1)}), bf16[16,32,768]{2,1,0:T(8,128)(2,1)S(1)}, u32[]{:S(2)}, u32[]{:S(2)}) async-start(bf16[16,32,768]{2,1,0:T(8,128)(2,1)} %pack_heads.1), calls=%async_computation | async-start | bytes 1572864 | tf_op jit(solution)/shard_map/all_to_all | solution.py:440
  10.3 0.0 copy-done.2
  10.3 0.5 collective-permute-start.1
  10.8 0.7 pad_add_fusion.place_ref
  11.5 17.5 %all-to-all-done.x_ref = bf16[16,32,768]{2,1,0:T(8,128)(2,1)S(1)} async-done(((bf16[16,32,768]{2,1,0:T(8,128)(2,1)}), bf16[16,32,768]{2,1,0:T(8,128)(2,1)S(1)}, u32[]{:S(2)}, u32[]{:S(2)}) %all-to-all-start) | async-done | bytes 786464 | tf_op jit(solution)/shard_map/all_to_all | solution.py:440
  29.0 0.0 copy-start.1
  29.0 0.9 copy-done.1
  29.9 2.6 %attend.1 = (bf16[2,192,128]{2,1,0:T(8,128)(2,1)}, bf16[2,192,128]{2,1,0:T(8,128)(2,1)}) custom-call(s32[2]{0:T(128)} %pad_add_fusion.place_ref, bf16[16,32,768]{2,1,0:T(8,128)(2,1)} %copy-done.1), custom_call_target="tpu_custom_call" | custom-call | tf_op jit(solution)/shard_map/attend/pallas_call | solution.py:252
  32.5 0.4 collective-permute-start
  32.9 1.2 %collective-permute-done = bf16[2,192,128]{2,1,0:T(8,128)(2,1)S(1)} collective-permute-done((bf16[2,192,128]{2,1,0:T(8,128)(2,1)}, bf16[2,192,128]{2,1,0:T(8,128)(2,1)S(1)}, u32[]{:S(2)}, u32[]{:S(2)}) %collective-permute-start) | collective-permute-done | bytes 98336 | tf_op jit(solution)/shard_map/ppermute | solution.py:385
  34.1 0.9 pad_maximum_fusion
  35.0 19.9 %all-gather = bf16[8,2,192,128]{3,2,1,0:T(8,128)(2,1)} all-gather(bf16[2,2,192,128]{3,2,1,0:T(8,128)(2,1)S(1)} %pad_maximum_fusion), channel_id=2, replica_groups=mesh['clip'=2,'seq'=4,'head'=4] {'seq'}, dimensions={0}, use_global_device_ids=true | all-gather | bytes 983040 | tf_op jit(solution)/shard_map/all_gather | solution.py:443
  54.9 0.0 collective-permute-done.1.refs_1_
  54.9 5.8 %project.1 = (bf16[4,32,1280]{2,1,0:T(8,128)(2,1)}, bf16[4,32,1280]{2,1,0:T(8,128)(2,1)}) custom-call(s32[1]{0:T(128)} %bitcast.me_ref, bf16[4,2,2,192,128]{4,3,2,1,0:T(8,128)(2,1)} %bitcast.26, bf16[768,1280]{1,0:T(8,128)(2,1)} %refs_0_.1, bf16[768,1280]{1,0:T(8,128)(2,1)} %collective-permute-done.1.refs_1_), custom_call_target="tpu_custom_call" | custom-call | tf_op jit(solution)/shard_map/project/pallas_call | solution.py:311
  60.7 0.0 copy-start.4
  60.7 1.4 %collective-permute-start.2 = (bf16[4,32,1280]{2,1,0:T(8,128)(2,1)}, bf16[4,32,1280]{2,1,0:T(8,128)(2,1)S(1)}, u32[]{:S(2)}, u32[]{:S(2)}) collective-permute-start(bf16[4,32,1280]{2,1,0:T(8,128)(2,1)} %get-tuple-element.11), channel_id=1, source_target_pairs={{0,2},{1,3},{2,0},{3,1},{4,6},{5,7},{6,4},{7,5},{8,10},{9,11},{10,... | collective-permute-start | bytes 983048 | tf_op jit(solution)/shard_map/ppermute | solution.py:448
  62.0 6.3 %collective-permute-done.2 = bf16[4,32,1280]{2,1,0:T(8,128)(2,1)S(1)} collective-permute-done((bf16[4,32,1280]{2,1,0:T(8,128)(2,1)}, bf16[4,32,1280]{2,1,0:T(8,128)(2,1)S(1)}, u32[]{:S(2)}, u32[]{:S(2)}) %collective-permute-start.2) | collective-permute-done | bytes 327712 | tf_op jit(solution)/shard_map/ppermute | solution.py:448
  68.4 1.8 %add_convert_fusion = bf16[4,32,1280]{2,1,0:T(8,128)(2,1)} fusion(bf16[4,32,1280]{2,1,0:T(8,128)(2,1)S(1)} %collective-permute-done.2, bf16[4,32,1280]{2,1,0:T(8,128)(2,1)} %get-tuple-element.10), kind=kLoop, calls=%fused_computation.1 | loop fusion | flops 655360 | bytes 983040 | tf_op jit(solution)/shard_map/convert_element_type | solution.py:449
  70.2 3.6 %all-to-all-start.1 = ((bf16[4,32,1280]{2,1,0:T(8,128)(2,1)}), bf16[4,32,1280]{2,1,0:T(8,128)(2,1)S(1)}, u32[]{:S(2)}, u32[]{:S(2)}) async-start(bf16[4,32,1280]{2,1,0:T(8,128)(2,1)} %add_convert_fusion), calls=%async_computation.1 | async-start | bytes 655360 | tf_op jit(solution)/shard_map/all_to_all | solution.py:450
  73.7 0.0 copy-done.4
  73.7 1.4 %copy.25.w_ref = bf16[5120,64]{1,0:T(8,128)(2,1)} copy(bf16[5120,64]{0,1:T(8,128)(2,1)S(1)} %copy-done.4) | data formatting | bytes 1310720 | tf_op args[8]
  75.1 5.9 %all-to-all-done.1.y_ref = bf16[4,32,1280]{2,1,0:T(8,128)(2,1)S(1)} async-done(((bf16[4,32,1280]{2,1,0:T(8,128)(2,1)}), bf16[4,32,1280]{2,1,0:T(8,128)(2,1)S(1)}, u32[]{:S(2)}, u32[]{:S(2)}) %all-to-all-start.1) | async-done | bytes 327712 | tf_op jit(solution)/shard_map/all_to_all | solution.py:450
  81.0 0.0 copy-start.3
  81.0 0.7 copy-done.3
  81.7 2.8 %finish.1 = (bf16[32,5120]{1,0:T(8,128)(2,1)}, bf16[32,64]{1,0:T(8,128)(2,1)}) custom-call(bf16[4,32,1280]{2,1,0:T(8,128)(2,1)} %copy-done.3, bf16[32,5120]{1,0:T(8,128)(2,1)} %bitcast.30, f32[1,5120]{1,0:T(1,128)} %bitcast.37, f32[1,5120]{1,0:T(1,128)} %bitcast.38, f32[1,5120]{1,0:T(1,128)} %bitcast.39, bf16[5120,64]{1,0:T(8,128)(2,1)} %copy.25.w_ref, ...), custom_call_target="tpu_custom_call" | custom-call | tf_op jit(solution)/shard_map/finish/pallas_call | solution.py:355
  84.5 0.0 copy-start.5
  84.5 1.4 %collective-permute-start.3 = (bf16[32,64]{1,0:T(8,128)(2,1)}, bf16[32,64]{1,0:T(8,128)(2,1)S(1)}, u32[]{:S(2)}, u32[]{:S(2)}) collective-permute-start(bf16[32,64]{1,0:T(8,128)(2,1)} %get-tuple-element.13), channel_id=1, source_target_pairs={{0,5},{1,6},{2,7},{4,9},{5,10},{6,11},{8,13},{9,14},{10,15},{16,21... | collective-permute-start | bytes 12296 | tf_op jit(solution)/shard_map/ppermute | solution.py:381
  85.9 5.3 %collective-permute-start.4 = (bf16[32,64]{1,0:T(8,128)(2,1)}, bf16[32,64]{1,0:T(8,128)(2,1)S(1)}, u32[]{:S(2)}, u32[]{:S(2)}) collective-permute-start(bf16[32,64]{1,0:T(8,128)(2,1)} %get-tuple-element.13), channel_id=1, source_target_pairs={{0,1},{1,2},{2,3},{4,5},{5,6},{6,7},{8,9},{9,10},{10,11},{12,13},{... | collective-permute-start | bytes 12296 | tf_op jit(solution)/shard_map/ppermute | solution.py:381
  91.2 0.7 collective-permute-start.5
  91.9 4.8 %collective-permute-start.6 = (bf16[32,64]{1,0:T(8,128)(2,1)}, bf16[32,64]{1,0:T(8,128)(2,1)S(1)}, u32[]{:S(2)}, u32[]{:S(2)}) collective-permute-start(bf16[32,64]{1,0:T(8,128)(2,1)} %get-tuple-element.13), channel_id=1, source_target_pairs={{0,4},{1,5},{2,6},{3,7},{4,8},{5,9},{6,10},{7,11},{8,12},{9,13},{1... | collective-permute-start | bytes 12296 | tf_op jit(solution)/shard_map/ppermute | solution.py:381
  96.7 1.3 %collective-permute-start.7 = (bf16[32,64]{1,0:T(8,128)(2,1)}, bf16[32,64]{1,0:T(8,128)(2,1)S(1)}, u32[]{:S(2)}, u32[]{:S(2)}) collective-permute-start(bf16[32,64]{1,0:T(8,128)(2,1)} %get-tuple-element.13), channel_id=1, source_target_pairs={{4,0},{5,1},{6,2},{7,3},{8,4},{9,5},{10,6},{11,7},{12,8},{13,9},{1... | collective-permute-start | bytes 12296 | tf_op jit(solution)/shard_map/ppermute | solution.py:381
  98.0 0.8 stack.58
  98.8 0.0 collective-permute-done.3
  98.8 0.1 stack.53
  98.8 0.0 collective-permute-done.4
  98.9 0.1 stack.54
  98.9 0.0 collective-permute-done.5
  99.0 0.1 stack.55
  99.0 0.0 collective-permute-done.6
  99.0 0.1 stack.57
  99.1 3.3 %collective-permute-done.7 = bf16[32,64]{1,0:T(8,128)(2,1)S(1)} collective-permute-done((bf16[32,64]{1,0:T(8,128)(2,1)}, bf16[32,64]{1,0:T(8,128)(2,1)S(1)}, u32[]{:S(2)}, u32[]{:S(2)}) %collective-permute-start.7) | collective-permute-done | bytes 4128 | tf_op jit(solution)/shard_map/ppermute | solution.py:381
  102.4 0.1 stack.59
  102.5 0.0 copy-start.6
  102.5 0.4 maximum_maximum_fusion
  102.9 0.2 copy.35
  103.2 0.1 pad_slice_fusion
  103.3 0.3 concatenate.6
  103.7 0.0 copy-done
  103.7 0.0 copy-done.5
  103.7 0.3 multiply_reduce_fusion
  104.0 0.0 copy-done.6
  104.0 0.8 multiply_convert_fusion
  (3 shorter events, 0.1 us)
Async XLA Ops:
  0.6 103.1 %copy-start = (bf16[3,3,3,16,384]{4,3,2,1,0:T(8,128)(2,1)S(1)}, bf16[3,3,3,16,384]{4,3,2,1,0:T(8,128)(2,1)}, u32[]{:S(2)}) copy-start(bf16[3,3,3,16,384]{4,3,2,1,0:T(8,128)(2,1)} %param.23) | copy-start | bytes 995332
  0.6 9.7 %copy-start.2 = (bf16[768,1280]{1,0:T(8,128)(2,1)S(1)}, bf16[768,1280]{1,0:T(8,128)(2,1)}, u32[]{:S(2)}) copy-start(bf16[768,1280]{1,0:T(8,128)(2,1)} %refs_0_.1) | copy-start | bytes 5898244
  2.9 26.1 %all-to-all-start = ((bf16[16,32,768]{2,1,0:T(8,128)(2,1)}), bf16[16,32,768]{2,1,0:T(8,128)(2,1)S(1)}, u32[]{:S(2)}, u32[]{:S(2)}) async-start(bf16[16,32,768]{2,1,0:T(8,128)(2,1)} %pack_heads.1), calls=%async_computation | async-start | bytes 1572864 | tf_op jit(solution)/shard_map/all_to_all | solution.py:440
  10.3 44.5 %collective-permute-start.1 = (bf16[768,1280]{1,0:T(8,128)(2,1)S(1)}, bf16[768,1280]{1,0:T(8,128)(2,1)}, u32[]{:S(2)}, u32[]{:S(2)}) collective-permute-start(bf16[768,1280]{1,0:T(8,128)(2,1)S(1)} %copy-done.2), channel_id=1, source_target_pairs={{0,1},{1,0},{2,3},{3,2},{4,5},{5,4},{6,7},{7,6},{8,9},{9,8},{10,11... | collective-permute-start | bytes 5898248 | tf_op jit(solution)/shard_map/ppermute | solution.py:385
  29.0 0.9 copy-start.1
  32.5 1.5 %collective-permute-start = (bf16[2,192,128]{2,1,0:T(8,128)(2,1)}, bf16[2,192,128]{2,1,0:T(8,128)(2,1)S(1)}, u32[]{:S(2)}, u32[]{:S(2)}) collective-permute-start(bf16[2,192,128]{2,1,0:T(8,128)(2,1)} %get-tuple-element.9), channel_id=1, source_target_pairs={{0,1},{1,0},{2,3},{3,2},{4,5},{5,4},{6,7},{7,6},{8,9},{9,8},{10,11... | collective-permute-start | bytes 294920 | tf_op jit(solution)/shard_map/ppermute | solution.py:385
  60.7 13.0 %copy-start.4 = (bf16[5120,64]{0,1:T(8,128)(2,1)S(1)}, bf16[5120,64]{0,1:T(8,128)(2,1)}, u32[]{:S(2)}) copy-start(bf16[5120,64]{0,1:T(8,128)(2,1)} %param.21) | copy-start | bytes 1966084
  60.7 7.7 %collective-permute-start.2 = (bf16[4,32,1280]{2,1,0:T(8,128)(2,1)}, bf16[4,32,1280]{2,1,0:T(8,128)(2,1)S(1)}, u32[]{:S(2)}, u32[]{:S(2)}) collective-permute-start(bf16[4,32,1280]{2,1,0:T(8,128)(2,1)} %get-tuple-element.11), channel_id=1, source_target_pairs={{0,2},{1,3},{2,0},{3,1},{4,6},{5,7},{6,4},{7,5},{8,10},{9,11},{10,... | collective-permute-start | bytes 983048 | tf_op jit(solution)/shard_map/ppermute | solution.py:448
  70.2 10.9 %all-to-all-start.1 = ((bf16[4,32,1280]{2,1,0:T(8,128)(2,1)}), bf16[4,32,1280]{2,1,0:T(8,128)(2,1)S(1)}, u32[]{:S(2)}, u32[]{:S(2)}) async-start(bf16[4,32,1280]{2,1,0:T(8,128)(2,1)} %add_convert_fusion), calls=%async_computation.1 | async-start | bytes 655360 | tf_op jit(solution)/shard_map/all_to_all | solution.py:450
  81.0 0.7 copy-start.3
  84.5 19.2 %copy-start.5 = (f32[384]{0:T(512)S(1)}, f32[384]{0:T(512)}, u32[]{:S(2)}) copy-start(f32[384]{0:T(512)} %param.24) | copy-start | bytes 4612
  84.5 14.3 %collective-permute-start.3 = (bf16[32,64]{1,0:T(8,128)(2,1)}, bf16[32,64]{1,0:T(8,128)(2,1)S(1)}, u32[]{:S(2)}, u32[]{:S(2)}) collective-permute-start(bf16[32,64]{1,0:T(8,128)(2,1)} %get-tuple-element.13), channel_id=1, source_target_pairs={{0,5},{1,6},{2,7},{4,9},{5,10},{6,11},{8,13},{9,14},{10,15},{16,21... | collective-permute-start | bytes 12296 | tf_op jit(solution)/shard_map/ppermute | solution.py:381
  85.9 12.9 %collective-permute-start.4 = (bf16[32,64]{1,0:T(8,128)(2,1)}, bf16[32,64]{1,0:T(8,128)(2,1)S(1)}, u32[]{:S(2)}, u32[]{:S(2)}) collective-permute-start(bf16[32,64]{1,0:T(8,128)(2,1)} %get-tuple-element.13), channel_id=1, source_target_pairs={{0,1},{1,2},{2,3},{4,5},{5,6},{6,7},{8,9},{9,10},{10,11},{12,13},{... | collective-permute-start | bytes 12296 | tf_op jit(solution)/shard_map/ppermute | solution.py:381
  91.2 7.7 %collective-permute-start.5 = (bf16[32,64]{1,0:T(8,128)(2,1)}, bf16[32,64]{1,0:T(8,128)(2,1)S(1)}, u32[]{:S(2)}, u32[]{:S(2)}) collective-permute-start(bf16[32,64]{1,0:T(8,128)(2,1)} %get-tuple-element.13), channel_id=1, source_target_pairs={{4,1},{5,2},{6,3},{8,5},{9,6},{10,7},{12,9},{13,10},{14,11},{20,17... | collective-permute-start | bytes 12296 | tf_op jit(solution)/shard_map/ppermute | solution.py:381
  91.9 7.2 %collective-permute-start.6 = (bf16[32,64]{1,0:T(8,128)(2,1)}, bf16[32,64]{1,0:T(8,128)(2,1)S(1)}, u32[]{:S(2)}, u32[]{:S(2)}) collective-permute-start(bf16[32,64]{1,0:T(8,128)(2,1)} %get-tuple-element.13), channel_id=1, source_target_pairs={{0,4},{1,5},{2,6},{3,7},{4,8},{5,9},{6,10},{7,11},{8,12},{9,13},{1... | collective-permute-start | bytes 12296 | tf_op jit(solution)/shard_map/ppermute | solution.py:381
  96.7 5.8 %collective-permute-start.7 = (bf16[32,64]{1,0:T(8,128)(2,1)}, bf16[32,64]{1,0:T(8,128)(2,1)S(1)}, u32[]{:S(2)}, u32[]{:S(2)}) collective-permute-start(bf16[32,64]{1,0:T(8,128)(2,1)} %get-tuple-element.13), channel_id=1, source_target_pairs={{4,0},{5,1},{6,2},{7,3},{8,4},{9,5},{10,6},{11,7},{12,8},{13,9},{1... | collective-permute-start | bytes 12296 | tf_op jit(solution)/shard_map/ppermute | solution.py:381
  102.5 1.5 %copy-start.6 = (f32[384]{0:T(512)S(1)}, f32[384]{0:T(512)}, u32[]{:S(2)}) copy-start(f32[384]{0:T(512)} %param.25) | copy-start | bytes 4612

commit v3 on v2

--- a/solution.py
+++ b/solution.py
@@ -261,7 +261,7 @@
     )(place.astype(jnp.int32), packed)
 
 
-def project_kernel_call(gathered, weights, seq_count, group, tokens):
+def project_kernel_call(gathered, weights, seq_count, group, tokens, step):
     whole, shared = divmod(group, seq_count)
     sharers = seq_count // shared if shared else 1
     part_rows = seq_count // sharers
@@ -269,45 +269,36 @@
     rows = seq_count * tokens
     width = weights[0].shape[1]
     block = width // 5 if width % 640 == 0 else width
-    me = (lax.axis_index("head") // 2).astype(jnp.int32).reshape(1)
-
-    def kernel(me_ref, x_ref, *refs):
-        w_refs = refs[: len(weights)]
-        out_refs = refs[len(weights) : -1]
-        a_ref = refs[-1]
+    far = ((lax.axis_index("head") // 2 + step) % outer).astype(jnp.int32).reshape(1)
+
+    def kernel(far_ref, x_ref, *refs):
+        w_refs, out_ref, a_ref = (refs[:-2], refs[-2], refs[-1])
 
         @pl.when(pl.program_id(0) == 0)
         def _():
-            for step in range(outer):
-                far = (me_ref[0] + step) % outer
-                base = step * rows
-                for seq in range(seq_count):
-                    for near in range(len(weights)):
-                        for slot in range(whole):
-                            col = (seq * whole + slot) * HEAD_DIM
-                            a_ref[near, base : base + rows, col : col + HEAD_DIM] = x_ref[
-                                seq, near, far, slot * rows : (slot + 1) * rows, :
-                            ]
-                        if shared:
-                            col = (whole * seq_count + seq // sharers) * HEAD_DIM
-                            to = base + (seq % sharers) * part_rows * tokens
-                            a_ref[
-                                near, to : to + part_rows * tokens, col : col + HEAD_DIM
-                            ] = x_ref[
-                                seq, near, far, whole * rows : (whole * rows + part_rows * tokens), :
-                            ]
+            at = far_ref[0]
+            for seq in range(seq_count):
+                for near in range(len(weights)):
+                    for slot in range(whole):
+                        col = (seq * whole + slot) * HEAD_DIM
+                        a_ref[near, :, col : col + HEAD_DIM] = x_ref[
+                            seq, near, at, slot * rows : (slot + 1) * rows, :
+                        ]
+                    if shared:
+                        col = (whole * seq_count + seq // sharers) * HEAD_DIM
+                        to = (seq % sharers) * part_rows * tokens
+                        a_ref[near, to : to + part_rows * tokens, col : col + HEAD_DIM] = x_ref[
+                            seq, near, at, whole * rows : (whole * rows + part_rows * tokens), :
+                        ]
 
         total = None
         for near, w_ref in enumerate(w_refs):
             term = jnp.dot(a_ref[near], w_ref[...], preferred_element_type=jnp.float32)
             total = term if total is None else total + term
         total = total.astype(jnp.bfloat16)
-        for step, out_ref in enumerate(out_refs):
-            for seq in range(seq_count):
-                at = step * rows + seq * tokens
-                out_ref[seq] = total[at : at + tokens]
-
-    out = jax.ShapeDtypeStruct((seq_count, tokens, width), jnp.bfloat16)
+        for seq in range(seq_count):
+            out_ref[seq] = total[seq * tokens : (seq + 1) * tokens]
+
     return pl.pallas_call(
         kernel,
         grid=(width // block,),
@@ -316,13 +307,16 @@
             pl.BlockSpec(gathered.shape, lambda i: (0, 0, 0, 0, 0)),
         ]
         + [pl.BlockSpec((w.shape[0], block), lambda i: (0, i)) for w in weights],
-        out_specs=[pl.BlockSpec((seq_count, tokens, block), lambda i: (0, 0, i))] * outer,
-        out_shape=[out] * outer,
-        scratch_shapes=[
-            pltpu.VMEM((len(weights), outer * rows, group * HEAD_DIM), jnp.bfloat16)
-        ],
-        name="project",
-    )(me, gathered, *weights)
+        out_specs=pl.BlockSpec((seq_count, tokens, block), lambda i: (0, 0, i)),
+        out_shape=jax.ShapeDtypeStruct((seq_count, tokens, width), jnp.bfloat16),
+        scratch_shapes=[pltpu.VMEM((len(weights), rows, group * HEAD_DIM), jnp.bfloat16)],
+        cost_estimate=pl.CostEstimate(
+            flops=2 * rows * group * HEAD_DIM * len(weights) * width,
+            bytes_accessed=2 * group * HEAD_DIM * len(weights) * width,
+            transcendentals=0,
+        ),
+        name="project_far" if step else "project_near",
+    )(far, gathered, *weights)
 
 
 def finish_kernel_call(columns, residual, gate, shift, scale, head_weight, head_bias):
@@ -370,15 +364,17 @@
     )
 
 
-def neighbour(value, seq_step, head_step):
-    seq_count, head_count = (lax.axis_size("seq"), lax.axis_size("head"))
-    pairs = []
-    for seq in range(seq_count):
-        for head in range(head_count):
-            to_seq, to_head = (seq + seq_step, head + head_step)
-            if 0 <= to_seq < seq_count and 0 <= to_head < head_count:
-                pairs.append((seq * head_count + head, to_seq * head_count + to_head))
-    return lax.ppermute(value, ("seq", "head"), pairs)
+def adjacent_rows(value):
+    count = lax.axis_size("seq")
+    mine = lax.axis_index("seq")
+
+    def exchange(first):
+        pairs = [(i, i + 1) for i in range(first, count - 1, 2)]
+        return lax.ppermute(value, "seq", pairs + [(j, i) for i, j in pairs])
+
+    even, odd = (exchange(0), exchange(1))
+    second = mine % 2 == 1
+    return (jnp.where(second, even, odd), jnp.where(second, odd, even))
 
 
 def swap_near(value, head_count):
@@ -441,11 +437,15 @@
     keep, send = attend_kernel_call(packed, seq_count, head_count, group)
     attended = jnp.stack([keep, swap_near(send, head_count)])
     gathered = lax.all_gather(attended, "seq", axis=0, tiled=False)
-    terms = project_kernel_call(gathered, weights, seq_count, group, tokens)
-    columns = terms[0].astype(jnp.float32)
+    received = []
     for step in range(1, head_count // 2):
         pairs = [(i, (i + 2 * step) % head_count) for i in range(head_count)]
-        columns = columns + lax.ppermute(terms[step], "head", pairs).astype(jnp.float32)
+        term = project_kernel_call(gathered, weights, seq_count, group, tokens, step)
+        received.append(lax.ppermute(term, "head", pairs))
+    columns = project_kernel_call(gathered, weights, seq_count, group, tokens, 0)
+    columns = columns.astype(jnp.float32)
+    for term in received:
+        columns = columns + term.astype(jnp.float32)
     columns = columns.astype(jnp.bfloat16)
     columns = lax.all_to_all(columns, "seq", split_axis=0, concat_axis=0, tiled=True)
     hidden, latent = finish_kernel_call(
@@ -457,10 +457,10 @@
         head_weight,
         head_bias,
     )
-    before = [neighbour(latent, step, 1) for step in (1, 0, -1)]
-    now = [neighbour(latent, 1, 0), latent, neighbour(latent, -1, 0)]
-    channels = latent.shape[1] // 4
-    grid = jnp.stack([jnp.stack(before), jnp.stack(now)]).reshape(
+    latent = jnp.stack([from_behind(latent, "head", 1), latent])
+    above, below = adjacent_rows(latent)
+    channels = latent.shape[-1] // 4
+    grid = jnp.stack([above, latent, below], 1).reshape(
         2, 3, frames, breadth, 2, 2, channels
     )
     video = grid.transpose(0, 2, 1, 4, 3, 5, 6).reshape(2 * frames, 6, 2 * breadth, channels)

time: 106 us -> 97.7 us (0.922)
  the two profiles are of different devices: /device:TPU:0 before, /device:TPU:10 now
where the time goes in v3:
time: 97.7 us; the launch traced here: 97 us
  waiting for transfers between devices  31.7 us (32%)
  starting transfers between devices  18.7 us (19%)
  Pallas kernels  18.3 us (19%)
  blocking collectives  17.5 us (18%)
  other arithmetic  5.13 us (5%)
  local copies, waits for them, and re-layouts  4.61 us (5%)
    all_to_all x1, waiting for transfers between devices, on_device(): lax.all_to_all(packed, ('seq', 'head'), split_axis=0, concat_axis=0, tile...  18.1 us
    all_gather x1, blocking collectives, on_device(): gathered = lax.all_gather(attended, 'seq', axis=0, tiled=False)  17.5 us
    pallas_call x2, Pallas kernels, project_kernel_call(): pl.pallas_call(kernel, grid=(width // block,), in_specs=[pl.BlockSpec(mem...  10.6 us
    all_to_all x1, starting transfers between devices, on_device(): lax.all_to_all(packed, ('seq', 'head'), split_axis=0, concat_axis=0, tile...  6.24 us
    all_to_all x1, starting transfers between devices, on_device(): lax.all_to_all(columns, 'seq', split_axis=0, concat_axis=0, tiled=True)  5.61 us
    all_to_all x1, waiting for transfers between devices, on_device(): lax.all_to_all(columns, 'seq', split_axis=0, concat_axis=0, tiled=True)  5.33 us
    ppermute x2, starting transfers between devices, exchange(): return lax.ppermute(value, 'seq', pairs + [(j, i) for i, j in pairs])  3.9 us
    ppermute x1, waiting for transfers between devices, from_behind(): lax.ppermute(value, axis, [(source, source + steps) for source in range(f...  3.25 us
  transfers between devices with their start and end apart: 8, of which 6 were waited for; matrix products, arithmetic and copies ran while one was open for 4% of the time, Pallas kernels for 8%

profile of v3, /device:TPU:10, one launch (start us, length us, event | category | flops | bytes accessed | tf_op | source)
XLA Modules:
  0.0 97.0 jit_solution(10149430584288192817)
XLA Ops:
  0.6 0.0 copy-start
  0.6 0.0 copy-start.1
  0.7 2.3 %pack_heads.1 = bf16[16,32,768]{2,1,0:T(8,128)(2,1)} custom-call(bf16[32,3072]{1,0:T(8,128)(2,1)} %bitcast.35, bf16[32,3072]{1,0:T(8,128)(2,1)} %bitcast.36, bf16[32,3072]{1,0:T(8,128)(2,1)} %bitcast.37), custom_call_target="tpu_custom_call" | custom-call | tf_op jit(solution)/shard_map/pack_heads/pallas_call | solution.py:202
  2.9 6.2 %all-to-all-start = ((bf16[16,32,768]{2,1,0:T(8,128)(2,1)}), bf16[16,32,768]{2,1,0:T(8,128)(2,1)S(1)}, u32[]{:S(2)}, u32[]{:S(2)}) async-start(bf16[16,32,768]{2,1,0:T(8,128)(2,1)} %pack_heads.1), calls=%async_computation | async-start | bytes 1572864 | tf_op jit(solution)/shard_map/all_to_all | solution.py:436
  9.2 0.0 copy-done.1
  9.2 0.2 collective-permute-start.1
  9.4 0.7 pad_add_fusion.place_ref
  10.0 18.1 %all-to-all-done.x_ref = bf16[16,32,768]{2,1,0:T(8,128)(2,1)S(1)} async-done(((bf16[16,32,768]{2,1,0:T(8,128)(2,1)}), bf16[16,32,768]{2,1,0:T(8,128)(2,1)S(1)}, u32[]{:S(2)}, u32[]{:S(2)}) %all-to-all-start) | async-done | bytes 786464 | tf_op jit(solution)/shard_map/all_to_all | solution.py:436
  28.1 0.0 copy-start.2
  28.1 0.9 copy-done.2
  29.0 2.6 %attend.1 = (bf16[2,192,128]{2,1,0:T(8,128)(2,1)}, bf16[2,192,128]{2,1,0:T(8,128)(2,1)}) custom-call(s32[2]{0:T(128)} %pad_add_fusion.place_ref, bf16[16,32,768]{2,1,0:T(8,128)(2,1)} %copy-done.2), custom_call_target="tpu_custom_call" | custom-call | tf_op jit(solution)/shard_map/attend/pallas_call | solution.py:252
  31.6 0.4 collective-permute-start
  32.0 1.2 %collective-permute-done = bf16[2,192,128]{2,1,0:T(8,128)(2,1)S(1)} collective-permute-done((bf16[2,192,128]{2,1,0:T(8,128)(2,1)}, bf16[2,192,128]{2,1,0:T(8,128)(2,1)S(1)}, u32[]{:S(2)}, u32[]{:S(2)}) %collective-permute-start) | collective-permute-done | bytes 98336 | tf_op jit(solution)/shard_map/ppermute | solution.py:381
  33.2 0.9 pad_maximum_fusion
  34.1 17.5 %all-gather = bf16[8,2,192,128]{3,2,1,0:T(8,128)(2,1)} all-gather(bf16[2,2,192,128]{3,2,1,0:T(8,128)(2,1)S(1)} %pad_maximum_fusion), channel_id=2, replica_groups=mesh['clip'=2,'seq'=4,'head'=4] {'seq'}, dimensions={0}, use_global_device_ids=true | all-gather | bytes 983040 | tf_op jit(solution)/shard_map/all_gather | solution.py:439
  51.6 0.0 collective-permute-done.1.refs_1_
  51.6 5.3 %project_far.1 = bf16[4,32,1280]{2,1,0:T(8,128)(2,1)} custom-call(s32[1]{0:T(128)} %bitcast.9.far_ref, bf16[4,2,2,192,128]{4,3,2,1,0:T(8,128)(2,1)} %bitcast.29, bf16[768,1280]{1,0:T(8,128)(2,1)} %refs_0_.3, bf16[768,1280]{1,0:T(8,128)(2,1)} %collective-permute-done.1.refs_1_), custom_call_target="tpu_custom_call" | custom-call | flops 503316480 | bytes 3932160 | tf_op jit(solution)/shard_map/project_far/pallas_call | solution.py:302
  56.9 0.3 collective-permute-start.2
  57.2 5.3 %project_near.1 = bf16[4,32,1280]{2,1,0:T(8,128)(2,1)} custom-call(s32[1]{0:T(128)} %bitcast.far_ref, bf16[4,2,2,192,128]{4,3,2,1,0:T(8,128)(2,1)} %bitcast.30, bf16[768,1280]{1,0:T(8,128)(2,1)} %refs_0_.3, bf16[768,1280]{1,0:T(8,128)(2,1)} %collective-permute-done.1.refs_1_), custom_call_target="tpu_custom_call" | custom-call | flops 503316480 | bytes 3932160 | tf_op jit(solution)/shard_map/project_near/pallas_call | solution.py:302
  62.5 0.0 copy-start.4
  62.5 2.5 %collective-permute-done.2 = bf16[4,32,1280]{2,1,0:T(8,128)(2,1)S(1)} collective-permute-done((bf16[4,32,1280]{2,1,0:T(8,128)(2,1)}, bf16[4,32,1280]{2,1,0:T(8,128)(2,1)S(1)}, u32[]{:S(2)}, u32[]{:S(2)}) %collective-permute-start.2) | collective-permute-done | bytes 327712 | tf_op jit(solution)/shard_map/ppermute | solution.py:444
  65.0 1.8 %add_convert_fusion = bf16[4,32,1280]{2,1,0:T(8,128)(2,1)} fusion(bf16[4,32,1280]{2,1,0:T(8,128)(2,1)S(1)} %collective-permute-done.2, bf16[4,32,1280]{2,1,0:T(8,128)(2,1)} %project_near.1), kind=kLoop, calls=%fused_computation.1 | loop fusion | flops 655360 | bytes 983040 | tf_op jit(solution)/shard_map/convert_element_type | solution.py:449
  66.8 5.6 %all-to-all-start.1 = ((bf16[4,32,1280]{2,1,0:T(8,128)(2,1)}), bf16[4,32,1280]{2,1,0:T(8,128)(2,1)S(1)}, u32[]{:S(2)}, u32[]{:S(2)}) async-start(bf16[4,32,1280]{2,1,0:T(8,128)(2,1)} %add_convert_fusion), calls=%async_computation.1 | async-start | bytes 655360 | tf_op jit(solution)/shard_map/all_to_all | solution.py:450
  72.4 0.0 copy-done.4
  72.4 1.4 %copy.25.w_ref = bf16[5120,64]{1,0:T(8,128)(2,1)} copy(bf16[5120,64]{0,1:T(8,128)(2,1)S(1)} %copy-done.4) | data formatting | bytes 1310720 | tf_op args[8]
  73.8 5.3 %all-to-all-done.1.y_ref = bf16[4,32,1280]{2,1,0:T(8,128)(2,1)S(1)} async-done(((bf16[4,32,1280]{2,1,0:T(8,128)(2,1)}), bf16[4,32,1280]{2,1,0:T(8,128)(2,1)S(1)}, u32[]{:S(2)}, u32[]{:S(2)}) %all-to-all-start.1) | async-done | bytes 327712 | tf_op jit(solution)/shard_map/all_to_all | solution.py:450
  79.2 0.0 copy-start.3
  79.2 0.7 copy-done.3
  79.9 2.8 %finish.1 = (bf16[32,5120]{1,0:T(8,128)(2,1)}, bf16[32,64]{1,0:T(8,128)(2,1)}) custom-call(bf16[4,32,1280]{2,1,0:T(8,128)(2,1)} %copy-done.3, bf16[32,5120]{1,0:T(8,128)(2,1)} %bitcast.34, f32[1,5120]{1,0:T(1,128)} %bitcast.43, f32[1,5120]{1,0:T(1,128)} %bitcast.44, f32[1,5120]{1,0:T(1,128)} %bitcast.45, bf16[5120,64]{1,0:T(8,128)(2,1)} %copy.25.w_ref, ...), custom_call_target="tpu_custom_call" | custom-call | tf_op jit(solution)/shard_map/finish/pallas_call | solution.py:349
  82.6 0.0 copy-start.5
  82.6 2.0 %collective-permute-start.3 = (bf16[32,64]{1,0:T(8,128)(2,1)}, bf16[32,64]{1,0:T(8,128)(2,1)S(1)}, u32[]{:S(2)}, u32[]{:S(2)}) collective-permute-start(bf16[32,64]{1,0:T(8,128)(2,1)} %get-tuple-element.9), channel_id=1, source_target_pairs={{0,1},{1,2},{2,3},{4,5},{5,6},{6,7},{8,9},{9,10},{10,11},{12,13},{... | collective-permute-start | bytes 12296 | tf_op jit(solution)/shard_map/ppermute | solution.py:14
  84.7 3.3 %collective-permute-done.3 = bf16[32,64]{1,0:T(8,128)(2,1)S(1)} collective-permute-done((bf16[32,64]{1,0:T(8,128)(2,1)}, bf16[32,64]{1,0:T(8,128)(2,1)S(1)}, u32[]{:S(2)}, u32[]{:S(2)}) %collective-permute-start.3) | collective-permute-done | bytes 4128 | tf_op jit(solution)/shard_map/ppermute | solution.py:14
  87.9 0.7 pad_maximum_fusion.3
  88.6 0.6 collective-permute-start.4
  89.2 3.3 %collective-permute-start.5 = (bf16[2,32,64]{2,1,0:T(8,128)(2,1)S(1)}, bf16[2,32,64]{2,1,0:T(8,128)(2,1)S(1)}, u32[]{:S(2)}, u32[]{:S(2)}) collective-permute-start(bf16[2,32,64]{2,1,0:T(8,128)(2,1)S(1)} %pad_maximum_fusion.3), channel_id=1, source_target_pairs={{4,8},{8,4},{5,9},{9,5},{6,10},{10,6},{7,11},{11,7},{20,24},{24,20... | collective-permute-start | bytes 24584 | tf_op jit(solution)/shard_map/ppermute | solution.py:373
  92.6 0.8 stack.54
  93.3 0.1 stack.53
  93.4 0.0 copy-start.6
  93.4 0.0 collective-permute-done.4
  93.5 1.4 %collective-permute-done.5 = bf16[2,32,64]{2,1,0:T(8,128)(2,1)S(1)} collective-permute-done((bf16[2,32,64]{2,1,0:T(8,128)(2,1)S(1)}, bf16[2,32,64]{2,1,0:T(8,128)(2,1)S(1)}, u32[]{:S(2)}, u32[]{:S(2)}) %collective-permute-start.5) | collective-permute-done | bytes 8224 | tf_op jit(solution)/shard_map/ppermute | solution.py:373
  94.8 0.1 stack.52
  94.9 0.1 stack.56
  95.0 0.3 pad_maximum_fusion.1
  95.4 0.1 pad_slice_fusion
  95.5 0.3 concatenate.5
  95.9 0.0 copy-done
  95.9 0.0 copy-done.5
  95.9 0.3 multiply_reduce_fusion
  96.2 0.0 copy-done.6
  96.2 0.8 multiply_convert_fusion
  (4 shorter events, 0.1 us)
Async XLA Ops:
  0.6 95.2 %copy-start = (bf16[3,3,3,16,384]{4,3,2,1,0:T(8,128)(2,1)S(1)}, bf16[3,3,3,16,384]{4,3,2,1,0:T(8,128)(2,1)}, u32[]{:S(2)}) copy-start(bf16[3,3,3,16,384]{4,3,2,1,0:T(8,128)(2,1)} %param.23) | copy-start | bytes 995332
  0.6 8.5 %copy-start.1 = (bf16[768,1280]{1,0:T(8,128)(2,1)S(1)}, bf16[768,1280]{1,0:T(8,128)(2,1)}, u32[]{:S(2)}) copy-start(bf16[768,1280]{1,0:T(8,128)(2,1)} %refs_0_.3) | copy-start | bytes 5898244
  2.9 25.2 %all-to-all-start = ((bf16[16,32,768]{2,1,0:T(8,128)(2,1)}), bf16[16,32,768]{2,1,0:T(8,128)(2,1)S(1)}, u32[]{:S(2)}, u32[]{:S(2)}) async-start(bf16[16,32,768]{2,1,0:T(8,128)(2,1)} %pack_heads.1), calls=%async_computation | async-start | bytes 1572864 | tf_op jit(solution)/shard_map/all_to_all | solution.py:436
  9.2 42.4 %collective-permute-start.1 = (bf16[768,1280]{1,0:T(8,128)(2,1)S(1)}, bf16[768,1280]{1,0:T(8,128)(2,1)}, u32[]{:S(2)}, u32[]{:S(2)}) collective-permute-start(bf16[768,1280]{1,0:T(8,128)(2,1)S(1)} %copy-done.1), channel_id=1, source_target_pairs={{0,1},{1,0},{2,3},{3,2},{4,5},{5,4},{6,7},{7,6},{8,9},{9,8},{10,11... | collective-permute-start | bytes 5898248 | tf_op jit(solution)/shard_map/ppermute | solution.py:381
  28.1 0.9 copy-start.2
  31.6 1.6 %collective-permute-start = (bf16[2,192,128]{2,1,0:T(8,128)(2,1)}, bf16[2,192,128]{2,1,0:T(8,128)(2,1)S(1)}, u32[]{:S(2)}, u32[]{:S(2)}) collective-permute-start(bf16[2,192,128]{2,1,0:T(8,128)(2,1)} %get-tuple-element.7), channel_id=1, source_target_pairs={{0,1},{1,0},{2,3},{3,2},{4,5},{5,4},{6,7},{7,6},{8,9},{9,8},{10,11... | collective-permute-start | bytes 294920 | tf_op jit(solution)/shard_map/ppermute | solution.py:381
  56.9 8.1 %collective-permute-start.2 = (bf16[4,32,1280]{2,1,0:T(8,128)(2,1)}, bf16[4,32,1280]{2,1,0:T(8,128)(2,1)S(1)}, u32[]{:S(2)}, u32[]{:S(2)}) collective-permute-start(bf16[4,32,1280]{2,1,0:T(8,128)(2,1)} %project_far.1), channel_id=1, source_target_pairs={{0,2},{1,3},{2,0},{3,1},{4,6},{5,7},{6,4},{7,5},{8,10},{9,11},{10,... | collective-permute-start | bytes 983048 | tf_op jit(solution)/shard_map/ppermute | solution.py:444
  62.5 9.9 %copy-start.4 = (bf16[5120,64]{0,1:T(8,128)(2,1)S(1)}, bf16[5120,64]{0,1:T(8,128)(2,1)}, u32[]{:S(2)}) copy-start(bf16[5120,64]{0,1:T(8,128)(2,1)} %param.21) | copy-start | bytes 1966084
  66.8 12.4 %all-to-all-start.1 = ((bf16[4,32,1280]{2,1,0:T(8,128)(2,1)}), bf16[4,32,1280]{2,1,0:T(8,128)(2,1)S(1)}, u32[]{:S(2)}, u32[]{:S(2)}) async-start(bf16[4,32,1280]{2,1,0:T(8,128)(2,1)} %add_convert_fusion), calls=%async_computation.1 | async-start | bytes 655360 | tf_op jit(solution)/shard_map/all_to_all | solution.py:450
  79.2 0.7 copy-start.3
  82.6 13.2 %copy-start.5 = (f32[384]{0:T(512)S(1)}, f32[384]{0:T(512)}, u32[]{:S(2)}) copy-start(f32[384]{0:T(512)} %param.24) | copy-start | bytes 4612
  82.6 5.3 %collective-permute-start.3 = (bf16[32,64]{1,0:T(8,128)(2,1)}, bf16[32,64]{1,0:T(8,128)(2,1)S(1)}, u32[]{:S(2)}, u32[]{:S(2)}) collective-permute-start(bf16[32,64]{1,0:T(8,128)(2,1)} %get-tuple-element.9), channel_id=1, source_target_pairs={{0,1},{1,2},{2,3},{4,5},{5,6},{6,7},{8,9},{9,10},{10,11},{12,13},{... | collective-permute-start | bytes 12296 | tf_op jit(solution)/shard_map/ppermute | solution.py:14
  88.6 4.8 %collective-permute-start.4 = (bf16[2,32,64]{2,1,0:T(8,128)(2,1)S(1)}, bf16[2,32,64]{2,1,0:T(8,128)(2,1)S(1)}, u32[]{:S(2)}, u32[]{:S(2)}) collective-permute-start(bf16[2,32,64]{2,1,0:T(8,128)(2,1)S(1)} %pad_maximum_fusion.3), channel_id=1, source_target_pairs={{0,4},{8,12},{4,0},{12,8},{1,5},{9,13},{5,1},{13,9},{2,6},{10,14},... | collective-permute-start | bytes 24584 | tf_op jit(solution)/shard_map/ppermute | solution.py:373
  89.2 5.6 %collective-permute-start.5 = (bf16[2,32,64]{2,1,0:T(8,128)(2,1)S(1)}, bf16[2,32,64]{2,1,0:T(8,128)(2,1)S(1)}, u32[]{:S(2)}, u32[]{:S(2)}) collective-permute-start(bf16[2,32,64]{2,1,0:T(8,128)(2,1)S(1)} %pad_maximum_fusion.3), channel_id=1, source_target_pairs={{4,8},{8,4},{5,9},{9,5},{6,10},{10,6},{7,11},{11,7},{20,24},{24,20... | collective-permute-start | bytes 24584 | tf_op jit(solution)/shard_map/ppermute | solution.py:373
  93.4 2.8 %copy-start.6 = (f32[384]{0:T(512)S(1)}, f32[384]{0:T(512)}, u32[]{:S(2)}) copy-start(f32[384]{0:T(512)} %param.25) | copy-start | bytes 4612

commit v4 on v3

--- a/solution.py
+++ b/solution.py
@@ -6,6 +6,7 @@
 from jax.sharding import PartitionSpec as P
 
 HEAD_DIM = 128
+KERNEL_VMEM = 24 * 2**20
 
 
 def from_behind(value, axis, steps):
@@ -204,6 +205,7 @@
         out_shape=jax.ShapeDtypeStruct(
             (seq_count * head_count, tokens, slots * 3 * HEAD_DIM), queries.dtype
         ),
+        compiler_params=pltpu.CompilerParams(vmem_limit_bytes=KERNEL_VMEM),
         name="pack_heads",
     )(queries, keys, values)
 
@@ -257,6 +259,7 @@
         ],
         out_shape=(half, half),
         scratch_shapes=[pltpu.VMEM((seq_count * head_count, tokens, HEAD_DIM), jnp.bfloat16)],
+        compiler_params=pltpu.CompilerParams(vmem_limit_bytes=KERNEL_VMEM),
         name="attend",
     )(place.astype(jnp.int32), packed)
 
@@ -274,40 +277,36 @@
     def kernel(far_ref, x_ref, *refs):
         w_refs, out_ref, a_ref = (refs[:-2], refs[-2], refs[-1])
 
-        @pl.when(pl.program_id(0) == 0)
-        def _():
-            at = far_ref[0]
+        at = far_ref[0]
+        for seq in range(seq_count):
+            for near in range(len(weights)):
+                for slot in range(whole):
+                    col = (seq * whole + slot) * HEAD_DIM
+                    a_ref[near, :, col : col + HEAD_DIM] = x_ref[
+                        seq, near, at, slot * rows : (slot + 1) * rows, :
+                    ]
+                if shared:
+                    col = (whole * seq_count + seq // sharers) * HEAD_DIM
+                    to = (seq % sharers) * part_rows * tokens
+                    a_ref[near, to : to + part_rows * tokens, col : col + HEAD_DIM] = x_ref[
+                        seq, near, at, whole * rows : (whole * rows + part_rows * tokens), :
+                    ]
+
+        for col in range(0, width, block):
+            total = None
+            for near, w_ref in enumerate(w_refs):
+                term = jnp.dot(
+                    a_ref[near], w_ref[:, col : col + block], preferred_element_type=jnp.float32
+                )
+                total = term if total is None else total + term
+            total = total.astype(jnp.bfloat16)
             for seq in range(seq_count):
-                for near in range(len(weights)):
-                    for slot in range(whole):
-                        col = (seq * whole + slot) * HEAD_DIM
-                        a_ref[near, :, col : col + HEAD_DIM] = x_ref[
-                            seq, near, at, slot * rows : (slot + 1) * rows, :
-                        ]
-                    if shared:
-                        col = (whole * seq_count + seq // sharers) * HEAD_DIM
-                        to = (seq % sharers) * part_rows * tokens
-                        a_ref[near, to : to + part_rows * tokens, col : col + HEAD_DIM] = x_ref[
-                            seq, near, at, whole * rows : (whole * rows + part_rows * tokens), :
-                        ]
-
-        total = None
-        for near, w_ref in enumerate(w_refs):
-            term = jnp.dot(a_ref[near], w_ref[...], preferred_element_type=jnp.float32)
-            total = term if total is None else total + term
-        total = total.astype(jnp.bfloat16)
-        for seq in range(seq_count):
-            out_ref[seq] = total[seq * tokens : (seq + 1) * tokens]
+                out_ref[seq, :, col : col + block] = total[seq * tokens : (seq + 1) * tokens]
 
     return pl.pallas_call(
         kernel,
-        grid=(width // block,),
-        in_specs=[
-            pl.BlockSpec(memory_space=pltpu.SMEM),
-            pl.BlockSpec(gathered.shape, lambda i: (0, 0, 0, 0, 0)),
-        ]
-        + [pl.BlockSpec((w.shape[0], block), lambda i: (0, i)) for w in weights],
-        out_specs=pl.BlockSpec((seq_count, tokens, block), lambda i: (0, 0, i)),
+        in_specs=[pl.BlockSpec(memory_space=pltpu.SMEM)]
+        + [pl.BlockSpec(memory_space=pltpu.VMEM)] * (1 + len(weights)),
         out_shape=jax.ShapeDtypeStruct((seq_count, tokens, width), jnp.bfloat16),
         scratch_shapes=[pltpu.VMEM((len(weights), rows, group * HEAD_DIM), jnp.bfloat16)],
         cost_estimate=pl.CostEstimate(
@@ -315,8 +314,24 @@
             bytes_accessed=2 * group * HEAD_DIM * len(weights) * width,
             transcendentals=0,
         ),
+        compiler_params=pltpu.CompilerParams(vmem_limit_bytes=KERNEL_VMEM),
         name="project_far" if step else "project_near",
     )(far, gathered, *weights)
+
+
+def add_terms(terms):
+    def kernel(*refs):
+        total = refs[0][...].astype(jnp.float32)
+        for ref in refs[1:-1]:
+            total = total + ref[...].astype(jnp.float32)
+        refs[-1][...] = total.astype(jnp.bfloat16)
+
+    return pl.pallas_call(
+        kernel,
+        out_shape=jax.ShapeDtypeStruct(terms[0].shape, jnp.bfloat16),
+        compiler_params=pltpu.CompilerParams(vmem_limit_bytes=KERNEL_VMEM),
+        name="add_terms",
+    )(*terms)
 
 
 def finish_kernel_call(columns, residual, gate, shift, scale, head_weight, head_bias):
@@ -352,6 +367,7 @@
             jax.ShapeDtypeStruct((tokens, model), jnp.bfloat16),
             jax.ShapeDtypeStruct((tokens, head_weight.shape[1]), jnp.bfloat16),
         ),
+        compiler_params=pltpu.CompilerParams(vmem_limit_bytes=KERNEL_VMEM),
         name="finish",
     )(
         columns,
@@ -443,10 +459,7 @@
         term = project_kernel_call(gathered, weights, seq_count, group, tokens, step)
         received.append(lax.ppermute(term, "head", pairs))
     columns = project_kernel_call(gathered, weights, seq_count, group, tokens, 0)
-    columns = columns.astype(jnp.float32)
-    for term in received:
-        columns = columns + term.astype(jnp.float32)
-    columns = columns.astype(jnp.bfloat16)
+    columns = add_terms([columns] + received)
     columns = lax.all_to_all(columns, "seq", split_axis=0, concat_axis=0, tiled=True)
     hidden, latent = finish_kernel_call(
         columns,

time: 97.7 us -> 91.8 us (0.940)
  Pallas kernels: 18.3 us -> 8.85 us
  waiting for transfers between devices: 31.7 us -> 38 us
  other arithmetic: 5.13 us -> 1.15 us
  starting transfers between devices: 18.7 us -> 19.7 us
    pallas_call x2 -> x3, Pallas kernels: 10.6 us -> 6.08 us  [the longest x2 5.28 us: project_kernel_call(): pl.pallas_call(kernel, in_specs=[pl.BlockSpec(memory_space=pltpu.SMEM)] +...]
    ppermute x1, waiting for transfers between devices: 2.49 us -> 6.21 us  [on_device(): received.append(lax.ppermute(term, 'head', pairs))]
    pallas_call x1, Pallas kernels: 2.27 us -> 0.12 us  [pack_heads(): pl.pallas_call(kernel, out_shape=jax.ShapeDtypeStruct((seq_count * head_c...]
    convert_element_type x1 -> x0, other arithmetic: 1.8 us -> none  [on_device(): columns = columns.astype(jnp.bfloat16)]
    ppermute x2, waiting for transfers between devices: 1.38 us -> 2.95 us  [exchange(): return lax.ppermute(value, 'seq', pairs + [(j, i) for i, j in pairs])]
    unnamed x15 -> x29, local copies, waits for them, and re-layouts: 3.04 us -> 4.61 us
    pallas_call x1, Pallas kernels: 2.75 us -> 1.29 us  [finish_kernel_call(): pl.pallas_call(kernel, out_shape=(jax.ShapeDtypeStruct((tokens, model), j...]
    pallas_call x1, Pallas kernels: 2.63 us -> 1.36 us  [attend_kernel_call(): pl.pallas_call(kernel, in_specs=[pl.BlockSpec(memory_space=pltpu.SMEM), p...]
  transfers between devices with their start and end apart: 8 -> 8, of which waited for: 6 -> 6; matrix products, arithmetic and copies ran while one was open for 4% -> 1% of each run, Pallas kernels for 8% -> 4%
where the time goes in v4:
time: 91.8 us; the launch traced here: 91.3 us
  waiting for transfers between devices  38 us (41%)
  starting transfers between devices  19.7 us (21%)
  blocking collectives  16.9 us (18%)
  Pallas kernels  8.85 us (10%)
  local copies, waits for them, and re-layouts  5.49 us (6%)
  other arithmetic  1.15 us (1%)
    all_to_all x1, waiting for transfers between devices, on_device(): lax.all_to_all(packed, ('seq', 'head'), split_axis=0, concat_axis=0, tile...  18.7 us
    all_gather x1, blocking collectives, on_device(): gathered = lax.all_gather(attended, 'seq', axis=0, tiled=False)  16.9 us
    all_to_all x1, starting transfers between devices, on_device(): lax.all_to_all(packed, ('seq', 'head'), split_axis=0, concat_axis=0, tile...  6.24 us
    ppermute x1, waiting for transfers between devices, on_device(): received.append(lax.ppermute(term, 'head', pairs))  6.21 us
    all_to_all x1, waiting for transfers between devices, on_device(): lax.all_to_all(columns, 'seq', split_axis=0, concat_axis=0, tiled=True)  6.17 us
    all_to_all x1, starting transfers between devices, on_device(): lax.all_to_all(columns, 'seq', split_axis=0, concat_axis=0, tiled=True)  5.61 us
    pallas_call x2, Pallas kernels, project_kernel_call(): pl.pallas_call(kernel, in_specs=[pl.BlockSpec(memory_space=pltpu.SMEM)] +...  5.28 us
    ppermute x2, starting transfers between devices, exchange(): return lax.ppermute(value, 'seq', pairs + [(j, i) for i, j in pairs])  4.7 us
  transfers between devices with their start and end apart: 8, of which 6 were waited for; matrix products, arithmetic and copies ran while one was open for 1% of the time, Pallas kernels for 4%

profile of v4, /device:TPU:10, one launch (start us, length us, event | category | flops | bytes accessed | tf_op | source)
XLA Modules:
  0.0 91.3 jit_solution(55768918579350766)
XLA Ops:
  0.6 0.0 copy-start
  0.6 0.0 copy-start.1
  0.7 0.0 copy-start.4
  0.7 1.1 %copy-done.4 = bf16[2,1,16,3072]{3,2,1,0:T(8,128)(2,1)S(1)} copy-done((bf16[2,1,16,3072]{3,2,1,0:T(8,128)(2,1)S(1)}, bf16[2,1,16,3072]{3,2,1,0:T(8,128)(2,1)}, u32[]{:S(2)}) %copy-start.4) | copy-done | bytes 196632
  1.7 0.0 copy-start.5
  1.7 0.9 %copy-done.5 = bf16[2,1,16,3072]{3,2,1,0:T(8,128)(2,1)S(1)} copy-done((bf16[2,1,16,3072]{3,2,1,0:T(8,128)(2,1)S(1)}, bf16[2,1,16,3072]{3,2,1,0:T(8,128)(2,1)}, u32[]{:S(2)}) %copy-start.5) | copy-done | bytes 196632
  2.7 0.0 copy-start.6
  2.7 0.9 %copy-done.6 = bf16[2,1,16,3072]{3,2,1,0:T(8,128)(2,1)S(1)} copy-done((bf16[2,1,16,3072]{3,2,1,0:T(8,128)(2,1)S(1)}, bf16[2,1,16,3072]{3,2,1,0:T(8,128)(2,1)}, u32[]{:S(2)}) %copy-start.6) | copy-done | bytes 196632
  3.6 0.1 pack_heads.1
  3.7 0.0 copy-start.2
  3.7 0.9 copy-done.2
  4.6 6.2 %all-to-all-start = ((bf16[16,32,768]{2,1,0:T(8,128)(2,1)}), bf16[16,32,768]{2,1,0:T(8,128)(2,1)S(1)}, u32[]{:S(2)}, u32[]{:S(2)}) async-start(bf16[16,32,768]{2,1,0:T(8,128)(2,1)} %copy-done.2), calls=%async_computation | async-start | bytes 1572864 | tf_op jit(solution)/shard_map/all_to_all | solution.py:452
  10.8 0.0 copy-done.1
  10.9 0.2 collective-permute-start.1
  11.0 0.1 pad_add_fusion.place_ref
  11.1 18.7 %all-to-all-done.x_ref = bf16[16,32,768]{2,1,0:T(8,128)(2,1)S(1)} async-done(((bf16[16,32,768]{2,1,0:T(8,128)(2,1)}), bf16[16,32,768]{2,1,0:T(8,128)(2,1)S(1)}, u32[]{:S(2)}, u32[]{:S(2)}) %all-to-all-start) | async-done | bytes 786464 | tf_op jit(solution)/shard_map/all_to_all | solution.py:452
  29.8 1.4 %attend.1 = (bf16[2,192,128]{2,1,0:T(8,128)(2,1)S(1)}, bf16[2,192,128]{2,1,0:T(8,128)(2,1)S(1)}) custom-call(s32[2]{0:T(128)S(1)} %pad_add_fusion.place_ref, bf16[16,32,768]{2,1,0:T(8,128)(2,1)S(1)} %all-to-all-done.x_ref), custom_call_target="tpu_custom_call" | custom-call | tf_op jit(solution)/shard_map/attend/pallas_call | solution.py:254
  31.2 0.5 collective-permute-start
  31.6 0.9 %collective-permute-done = bf16[2,192,128]{2,1,0:T(8,128)(2,1)S(1)} collective-permute-done((bf16[2,192,128]{2,1,0:T(8,128)(2,1)S(1)}, bf16[2,192,128]{2,1,0:T(8,128)(2,1)S(1)}, u32[]{:S(2)}, u32[]{:S(2)}) %collective-permute-start) | collective-permute-done | bytes 98336 | tf_op jit(solution)/shard_map/ppermute | solution.py:397
  32.6 16.9 %all-gather = bf16[8,2,192,128]{3,2,1,0:T(8,128)(2,1)S(1)} all-gather(bf16[2,2,192,128]{3,2,1,0:T(8,128)(2,1)S(1)} %pad_maximum_fusion), channel_id=2, replica_groups=mesh['clip'=2,'seq'=4,'head'=4] {'seq'}, dimensions={0}, use_global_device_ids=true | all-gather | bytes 983040 | tf_op jit(solution)/shard_map/all_gather | solution.py:455
  49.5 0.0 collective-permute-done.1.refs_1_
  49.5 3.0 %project_far.1 = bf16[4,32,1280]{2,1,0:T(8,128)(2,1)} custom-call(s32[1]{0:T(128)} %bitcast.9.far_ref, bf16[4,2,2,192,128]{4,3,2,1,0:T(8,128)(2,1)S(1)} %bitcast.29, bf16[768,1280]{1,0:T(8,128)(2,1)S(1)} %copy-done.1, bf16[768,1280]{1,0:T(8,128)(2,1)} %collective-permute-done.1.refs_1_), custom_call_target="tpu_custom_call" | custom-call | flops 503316480 | bytes 3932160 | tf_op jit(solution)/shard_map/project_far/pallas_call | solution.py:306
  52.5 0.5 collective-permute-start.2
  53.0 2.3 %project_near.1.refs_0_ = bf16[4,32,1280]{2,1,0:T(8,128)(2,1)S(1)} custom-call(s32[1]{0:T(128)} %bitcast.far_ref, bf16[4,2,2,192,128]{4,3,2,1,0:T(8,128)(2,1)S(1)} %bitcast.30, bf16[768,1280]{1,0:T(8,128)(2,1)S(1)} %copy-done.1, bf16[768,1280]{1,0:T(8,128)(2,1)} %collective-permute-done.1.refs_1_), custom_call_target="tpu_custom_call" | custom-call | flops 503316480 | bytes 3932160 | tf_op jit(solution)/shard_map/project_near/pallas_call | solution.py:306
  55.2 0.0 copy-start.11
  55.3 0.0 copy-start.3
  55.3 0.0 copy-start.7
  55.3 0.0 copy-start.8
  55.3 0.0 copy-start.9
  55.3 0.0 copy-start.10
  55.3 6.2 %collective-permute-done.2.refs_1_ = bf16[4,32,1280]{2,1,0:T(8,128)(2,1)S(1)} collective-permute-done((bf16[4,32,1280]{2,1,0:T(8,128)(2,1)}, bf16[4,32,1280]{2,1,0:T(8,128)(2,1)S(1)}, u32[]{:S(2)}, u32[]{:S(2)}) %collective-permute-start.2) | collective-permute-done | bytes 327712 | tf_op jit(solution)/shard_map/ppermute | solution.py:460
  61.5 0.8 add_terms.1
  62.3 5.6 %all-to-all-start.1 = ((bf16[4,32,1280]{2,1,0:T(8,128)(2,1)}), bf16[4,32,1280]{2,1,0:T(8,128)(2,1)S(1)}, u32[]{:S(2)}, u32[]{:S(2)}) async-start(bf16[4,32,1280]{2,1,0:T(8,128)(2,1)} %add_terms.1), calls=%async_computation.1 | async-start | bytes 655360 | tf_op jit(solution)/shard_map/all_to_all | solution.py:463
  67.9 0.0 copy-done.11
  67.9 0.7 copy.25.w_ref
  68.7 6.2 %all-to-all-done.1.y_ref = bf16[4,32,1280]{2,1,0:T(8,128)(2,1)S(1)} async-done(((bf16[4,32,1280]{2,1,0:T(8,128)(2,1)}), bf16[4,32,1280]{2,1,0:T(8,128)(2,1)S(1)}, u32[]{:S(2)}, u32[]{:S(2)}) %all-to-all-start.1) | async-done | bytes 327712 | tf_op jit(solution)/shard_map/all_to_all | solution.py:463
  74.9 0.0 copy-done.3
  74.9 0.0 copy-done.7
  74.9 0.0 copy-done.8
  74.9 0.0 copy-done.9
  74.9 0.0 copy-done.10
  74.9 1.3 %finish.1 = (bf16[32,5120]{1,0:T(8,128)(2,1)}, bf16[32,64]{1,0:T(8,128)(2,1)S(1)}) custom-call(bf16[4,32,1280]{2,1,0:T(8,128)(2,1)S(1)} %all-to-all-done.1.y_ref, bf16[32,5120]{1,0:T(8,128)(2,1)S(1)} %bitcast.31, f32[1,5120]{1,0:T(1,128)S(1)} %bitcast.37, f32[1,5120]{1,0:T(1,128)S(1)} %bitcast.38, f32[1,5120]{1,0:T(1,128)S(1)} %bitcast.39, ...), custom_call_target="tpu_custom_call" | custom-call | tf_op jit(solution)/shard_map/finish/pallas_call | solution.py:364
  76.2 0.0 copy-start.12
  76.2 2.0 %collective-permute-start.3 = (bf16[32,64]{1,0:T(8,128)(2,1)S(1)}, bf16[32,64]{1,0:T(8,128)(2,1)S(1)}, u32[]{:S(2)}, u32[]{:S(2)}) collective-permute-start(bf16[32,64]{1,0:T(8,128)(2,1)S(1)} %get-tuple-element.9), channel_id=1, source_target_pairs={{0,1},{1,2},{2,3},{4,5},{5,6},{6,7},{8,9},{9,10},{10,11},{12,13},{... | collective-permute-start | bytes 12296 | tf_op jit(solution)/shard_map/ppermute | solution.py:15
  78.2 3.0 %collective-permute-done.3 = bf16[32,64]{1,0:T(8,128)(2,1)S(1)} collective-permute-done((bf16[32,64]{1,0:T(8,128)(2,1)S(1)}, bf16[32,64]{1,0:T(8,128)(2,1)S(1)}, u32[]{:S(2)}, u32[]{:S(2)}) %collective-permute-start.3) | collective-permute-done | bytes 4128 | tf_op jit(solution)/shard_map/ppermute | solution.py:15
  81.3 2.2 %collective-permute-start.4 = (bf16[2,32,64]{2,1,0:T(8,128)(2,1)S(1)}, bf16[2,32,64]{2,1,0:T(8,128)(2,1)S(1)}, u32[]{:S(2)}, u32[]{:S(2)}) collective-permute-start(bf16[2,32,64]{2,1,0:T(8,128)(2,1)S(1)} %pad_maximum_fusion.3), channel_id=1, source_target_pairs={{0,4},{8,12},{4,0},{12,8},{1,5},{9,13},{5,1},{13,9},{2,6},{10,14},... | collective-permute-start | bytes 24584 | tf_op jit(solution)/shard_map/ppermute | solution.py:389
  83.5 2.5 %collective-permute-start.5 = (bf16[2,32,64]{2,1,0:T(8,128)(2,1)S(1)}, bf16[2,32,64]{2,1,0:T(8,128)(2,1)S(1)}, u32[]{:S(2)}, u32[]{:S(2)}) collective-permute-start(bf16[2,32,64]{2,1,0:T(8,128)(2,1)S(1)} %pad_maximum_fusion.3), channel_id=1, source_target_pairs={{4,8},{8,4},{5,9},{9,5},{6,10},{10,6},{7,11},{11,7},{20,24},{24,20... | collective-permute-start | bytes 24584 | tf_op jit(solution)/shard_map/ppermute | solution.py:389
  86.0 0.1 stack.54
  86.1 0.1 stack.53
  86.2 0.0 copy-start.13
  86.2 0.0 collective-permute-done.4
  86.2 3.0 %collective-permute-done.5 = bf16[2,32,64]{2,1,0:T(8,128)(2,1)S(1)} collective-permute-done((bf16[2,32,64]{2,1,0:T(8,128)(2,1)S(1)}, bf16[2,32,64]{2,1,0:T(8,128)(2,1)S(1)}, u32[]{:S(2)}, u32[]{:S(2)}) %collective-permute-start.5) | collective-permute-done | bytes 8224 | tf_op jit(solution)/shard_map/ppermute | solution.py:389
  89.2 0.1 stack.52
  89.3 0.1 stack.56
  89.4 0.3 pad_maximum_fusion.1
  89.7 0.1 pad_slice_fusion
  89.8 0.3 concatenate.5
  90.2 0.0 copy-done
  90.2 0.0 copy-done.12
  90.2 0.3 multiply_reduce_fusion
  90.5 0.0 copy-done.13
  90.5 0.8 multiply_convert_fusion
  (6 shorter events, 0.1 us)
Async XLA Ops:
  0.6 89.6 %copy-start = (bf16[3,3,3,16,384]{4,3,2,1,0:T(8,128)(2,1)S(1)}, bf16[3,3,3,16,384]{4,3,2,1,0:T(8,128)(2,1)}, u32[]{:S(2)}) copy-start(bf16[3,3,3,16,384]{4,3,2,1,0:T(8,128)(2,1)} %param.23) | copy-start | bytes 995332
  0.6 10.2 %copy-start.1 = (bf16[768,1280]{1,0:T(8,128)(2,1)S(1)}, bf16[768,1280]{1,0:T(8,128)(2,1)}, u32[]{:S(2)}) copy-start(bf16[768,1280]{1,0:T(8,128)(2,1)} %refs_0_.3) | copy-start | bytes 5898244
  0.7 1.1 %copy-start.4 = (bf16[2,1,16,3072]{3,2,1,0:T(8,128)(2,1)S(1)}, bf16[2,1,16,3072]{3,2,1,0:T(8,128)(2,1)}, u32[]{:S(2)}) copy-start(bf16[2,1,16,3072]{3,2,1,0:T(8,128)(2,1)} %param.13) | copy-start | bytes 589828
  1.7 0.9 %copy-start.5 = (bf16[2,1,16,3072]{3,2,1,0:T(8,128)(2,1)S(1)}, bf16[2,1,16,3072]{3,2,1,0:T(8,128)(2,1)}, u32[]{:S(2)}) copy-start(bf16[2,1,16,3072]{3,2,1,0:T(8,128)(2,1)} %param.14) | copy-start | bytes 589828
  2.7 0.9 %copy-start.6 = (bf16[2,1,16,3072]{3,2,1,0:T(8,128)(2,1)S(1)}, bf16[2,1,16,3072]{3,2,1,0:T(8,128)(2,1)}, u32[]{:S(2)}) copy-start(bf16[2,1,16,3072]{3,2,1,0:T(8,128)(2,1)} %param.15) | copy-start | bytes 589828
  3.7 0.9 copy-start.2
  4.6 25.2 %all-to-all-start = ((bf16[16,32,768]{2,1,0:T(8,128)(2,1)}), bf16[16,32,768]{2,1,0:T(8,128)(2,1)S(1)}, u32[]{:S(2)}, u32[]{:S(2)}) async-start(bf16[16,32,768]{2,1,0:T(8,128)(2,1)} %copy-done.2), calls=%async_computation | async-start | bytes 1572864 | tf_op jit(solution)/shard_map/all_to_all | solution.py:452
  10.9 38.6 %collective-permute-start.1 = (bf16[768,1280]{1,0:T(8,128)(2,1)S(1)}, bf16[768,1280]{1,0:T(8,128)(2,1)}, u32[]{:S(2)}, u32[]{:S(2)}) collective-permute-start(bf16[768,1280]{1,0:T(8,128)(2,1)S(1)} %copy-done.1), channel_id=1, source_target_pairs={{0,1},{1,0},{2,3},{3,2},{4,5},{5,4},{6,7},{7,6},{8,9},{9,8},{10,11... | collective-permute-start | bytes 5898248 | tf_op jit(solution)/shard_map/ppermute | solution.py:397
  31.2 1.4 %collective-permute-start = (bf16[2,192,128]{2,1,0:T(8,128)(2,1)S(1)}, bf16[2,192,128]{2,1,0:T(8,128)(2,1)S(1)}, u32[]{:S(2)}, u32[]{:S(2)}) collective-permute-start(bf16[2,192,128]{2,1,0:T(8,128)(2,1)S(1)} %get-tuple-element.7), channel_id=1, source_target_pairs={{0,1},{1,0},{2,3},{3,2},{4,5},{5,4},{6,7},{7,6},{8,9},{9,8},{10,11... | collective-permute-start | bytes 294920 | tf_op jit(solution)/shard_map/ppermute | solution.py:397
  52.5 9.1 %collective-permute-start.2 = (bf16[4,32,1280]{2,1,0:T(8,128)(2,1)}, bf16[4,32,1280]{2,1,0:T(8,128)(2,1)S(1)}, u32[]{:S(2)}, u32[]{:S(2)}) collective-permute-start(bf16[4,32,1280]{2,1,0:T(8,128)(2,1)} %project_far.1), channel_id=1, source_target_pairs={{0,2},{1,3},{2,0},{3,1},{4,6},{5,7},{6,4},{7,5},{8,10},{9,11},{10,... | collective-permute-start | bytes 983048 | tf_op jit(solution)/shard_map/ppermute | solution.py:460
  55.2 12.7 %copy-start.11 = (bf16[5120,64]{0,1:T(8,128)(2,1)S(1)}, bf16[5120,64]{0,1:T(8,128)(2,1)}, u32[]{:S(2)}) copy-start(bf16[5120,64]{0,1:T(8,128)(2,1)} %param.21) | copy-start | bytes 1966084
  55.3 19.6 %copy-start.3 = (bf16[2,1,16,5120]{3,2,1,0:T(8,128)(2,1)S(1)}, bf16[2,1,16,5120]{3,2,1,0:T(8,128)(2,1)}, u32[]{:S(2)}) copy-start(bf16[2,1,16,5120]{3,2,1,0:T(8,128)(2,1)} %param.16) | copy-start | bytes 983044
  55.3 19.6 %copy-start.7 = (f32[5120]{0:T(1024)S(1)}, f32[5120]{0:T(1024)}, u32[]{:S(2)}) copy-start(f32[5120]{0:T(1024)} %param.18) | copy-start | bytes 61444
  55.3 19.6 %copy-start.8 = (f32[5120]{0:T(1024)S(1)}, f32[5120]{0:T(1024)}, u32[]{:S(2)}) copy-start(f32[5120]{0:T(1024)} %param.19) | copy-start | bytes 61444
  55.3 19.6 %copy-start.9 = (f32[5120]{0:T(1024)S(1)}, f32[5120]{0:T(1024)}, u32[]{:S(2)}) copy-start(f32[5120]{0:T(1024)} %param.20) | copy-start | bytes 61444
  55.3 19.6 %copy-start.10 = (f32[64]{0:T(128)S(1)}, f32[64]{0:T(128)}, u32[]{:S(2)}) copy-start(f32[64]{0:T(128)} %param.22) | copy-start | bytes 772
  62.3 12.5 %all-to-all-start.1 = ((bf16[4,32,1280]{2,1,0:T(8,128)(2,1)}), bf16[4,32,1280]{2,1,0:T(8,128)(2,1)S(1)}, u32[]{:S(2)}, u32[]{:S(2)}) async-start(bf16[4,32,1280]{2,1,0:T(8,128)(2,1)} %add_terms.1), calls=%async_computation.1 | async-start | bytes 655360 | tf_op jit(solution)/shard_map/all_to_all | solution.py:463
  76.2 14.0 %copy-start.12 = (f32[384]{0:T(512)S(1)}, f32[384]{0:T(512)}, u32[]{:S(2)}) copy-start(f32[384]{0:T(512)} %param.24) | copy-start | bytes 4612
  76.2 5.1 %collective-permute-start.3 = (bf16[32,64]{1,0:T(8,128)(2,1)S(1)}, bf16[32,64]{1,0:T(8,128)(2,1)S(1)}, u32[]{:S(2)}, u32[]{:S(2)}) collective-permute-start(bf16[32,64]{1,0:T(8,128)(2,1)S(1)} %get-tuple-element.9), channel_id=1, source_target_pairs={{0,1},{1,2},{2,3},{4,5},{5,6},{6,7},{8,9},{9,10},{10,11},{12,13},{... | collective-permute-start | bytes 12296 | tf_op jit(solution)/shard_map/ppermute | solution.py:15
  81.3 4.9 %collective-permute-start.4 = (bf16[2,32,64]{2,1,0:T(8,128)(2,1)S(1)}, bf16[2,32,64]{2,1,0:T(8,128)(2,1)S(1)}, u32[]{:S(2)}, u32[]{:S(2)}) collective-permute-start(bf16[2,32,64]{2,1,0:T(8,128)(2,1)S(1)} %pad_maximum_fusion.3), channel_id=1, source_target_pairs={{0,4},{8,12},{4,0},{12,8},{1,5},{9,13},{5,1},{13,9},{2,6},{10,14},... | collective-permute-start | bytes 24584 | tf_op jit(solution)/shard_map/ppermute | solution.py:389
  83.5 5.6 %collective-permute-start.5 = (bf16[2,32,64]{2,1,0:T(8,128)(2,1)S(1)}, bf16[2,32,64]{2,1,0:T(8,128)(2,1)S(1)}, u32[]{:S(2)}, u32[]{:S(2)}) collective-permute-start(bf16[2,32,64]{2,1,0:T(8,128)(2,1)S(1)} %pad_maximum_fusion.3), channel_id=1, source_target_pairs={{4,8},{8,4},{5,9},{9,5},{6,10},{10,6},{7,11},{11,7},{20,24},{24,20... | collective-permute-start | bytes 24584 | tf_op jit(solution)/shard_map/ppermute | solution.py:389
  86.2 4.4 %copy-start.13 = (f32[384]{0:T(512)S(1)}, f32[384]{0:T(512)}, u32[]{:S(2)}) copy-start(f32[384]{0:T(512)} %param.25) | copy-start | bytes 4612
